TPU v7x, 32 devices: a whole 2x2x4 slice. The times are simulated.
32 devices in a mesh: gx: 4 (over y, x), gy: 4 (over z), layer: 2 (over core).
Axes of the slice: x: 2, y: 2, z: 4, core: 2. Of those that a mesh axis runs over, the one named last changes fastest.
Arguments:
- profiles: bfloat16 [2, 4, 65536, 256], P('layer', 'gx', 'gy'), may hold values from 0.049804688 to 2
- time_weight: bfloat16 [256], replicated, may hold values from 0 to 0.029907227
- slot_cell: int32 [2, 4, 65536], P('layer', 'gx', 'gy'), may hold values from 0 to 65535
- inst_count: int32 [2, 4, 4], P('layer', 'gx', 'gy'), may hold values from 1 to 16384, as said below
- metal: float32 [6, 512, 2048], P('layer', 'gx', 'gy'), may hold values from 0.5 to 4
- via_density: float32 [512, 2048], P('gx', 'gy'), may hold values from 0.5 to 4
- pad: float32 [512, 2048], P('gx', 'gy'), may hold values from 0.05 to 0.5
- start_drop: float32 [6, 512, 2048], P('layer', 'gx', 'gy'), may hold values from 0 to 1
Outputs:
- drop: float32 [6, 512, 2048], P('layer', 'gx', 'gy')
- residual: float32 [6, 512, 2048], P('layer', 'gx', 'gy')
Inputs may be any that keep to these rules, and one draw needn't show every extreme that they name: The first inst_count slots of a device are live, the rest are padding; and one device is full in every draw. `slot_cell`: row-major cell index within the tile of 128 x 512 cells.
All inputs are finite; a program needn't handle non-finite values.
Results may differ from a plain program's by a relative error of at most 0.0018.
Values sent between devices are 32-bit elements; how exact they have to be, the bound alone decides.
A program may use at most 64 MiB of HBM per device.

v0:
```python
import functools

import jax
import jax.numpy as jnp
from jax import lax
from jax.experimental import pallas as pl
from jax.experimental.pallas import tpu as pltpu
from jax.sharding import PartitionSpec as P

ITERS = 3
PAD = 8
LANES = 128
WIDE = 256
BARRIER_AT = 6
MESH = pl.DeviceIdType.MESH


def harmonic(values, beside):
    return 2.0 * values * beside / (values + beside)


def div_by(values, size):
    if size & (size - 1) == 0:
        return lax.shift_right_logical(values, jnp.full_like(values, size.bit_length() - 1))
    return lax.div(values, size)


def rem_by(values, size):
    return values & (size - 1) if size & (size - 1) == 0 else lax.rem(values, size)


def cg_coefficients(moments):
    def form(left, right):
        total = None
        for a, x in enumerate(left):
            for b, y in enumerate(right):
                term = x * y * moments[a + b]
                total = term if total is None else total + term
        return total

    one = jnp.ones_like(moments[0])
    scaled, direction = [one], [one]
    moved = [jnp.zeros_like(one)] * ITERS
    energy = form(scaled, scaled)
    for iteration in range(ITERS):
        image = [
            (direction[c] if c < len(direction) else 0.0) - (direction[c - 1] if c else 0.0)
            for c in range(len(direction) + 1)
        ]
        step = energy / form(direction, image)
        for c, value in enumerate(direction):
            moved[c] = moved[c] + step * value
        scaled = [
            (scaled[c] if c < len(scaled) else 0.0) - step * image[c] for c in range(len(image))
        ]
        if iteration + 1 < ITERS:
            energy_next = form(scaled, scaled)
            momentum = energy_next / energy
            direction = [
                scaled[c] + (momentum * direction[c] if c < len(direction) else 0.0)
                for c in range(len(scaled))
            ]
            energy = energy_next
    return moved, scaled


def kernel(
    sizes, slots, profiles, weight_in, cells_in, count, metal_in, via_in, pad_in, start_in, drop, residual,
    weight, cells, metal, via, pad, start, isem, pbuf, psem, acc, cur_recv, dinv, diag, coef, field, rows_send, rows_recv, cols_pack, cols_send, cols_recv,
    plane_recv, col_halo, sums, gather, send_sem, recv_sem, gsend, grecv,
):
    ngx, ngy, nlayer = sizes
    total = ngx * ngy * nlayer
    nl, nr, nc = metal.shape
    gx, gy, layer = lax.axis_index("gx"), lax.axis_index("gy"), lax.axis_index("layer")
    me = (gx * ngy + gy) * nlayer + layer
    chunks = pbuf.shape[0]

    def coords(flat):
        return (flat // (ngy * nlayer), (flat // nlayer) % ngy, flat % nlayer)

    loads = [
        pltpu.make_async_copy(src, dst, isem.at[i])
        for i, (src, dst) in enumerate(
            ((cells_in, cells), (metal_in, metal), (start_in, start), (via_in, via), (pad_in, pad), (weight_in, weight))
        )
    ]
    chunk_loads = [pltpu.make_async_copy(profiles.at[i], pbuf.at[i], psem.at[i]) for i in range(chunks)]
    for op in loads[1:3] + loads[5:] + loads[:1] + chunk_loads + loads[3:5]:
        op.start()
    barrier = pltpu.get_barrier_semaphore()

    def other(at, offset, size):
        return at ^ offset if size & (size - 1) == 0 else lax.rem(at + offset, size)

    def peers(visit):
        if total <= 64:
            offsets = [(a, b, c) for a in range(ngx) for b in range(ngy) for c in range(nlayer)]
            for a, b, c in sorted(offsets[1:], key=lambda o: -(o[0].bit_count() + o[1] + 0.5 * o[2])):
                visit((other(gx, a, ngx), other(gy, b, ngy), other(layer, c, nlayer)))
        else:
            def one(k, carry):
                visit(coords(lax.rem(me + k, total)))
                return carry

            lax.fori_loop(1, total, one, 0)

    peers(lambda device: pl.semaphore_signal(barrier, inc=1, device_id=device, device_id_type=MESH))

    lane = lax.broadcasted_iota(jnp.int32, (nr, LANES), 1)

    def pack_columns(first_of, last_of, count_of):
        packed = jnp.zeros((nr, LANES), jnp.float32)
        for l in range(count_of):
            packed = jnp.where(lane == l, last_of(l), packed)
            packed = jnp.where(lane == 8 + l, first_of(l), packed)
        return packed

    def exchange(e):
        own = layer
        def copy(src, dst, k, device):
            return pltpu.make_async_remote_copy(
                src_ref=src, dst_ref=dst, send_sem=send_sem.at[e, k], recv_sem=recv_sem.at[e, k],
                device_id=device, device_id_type=MESH,
            )
        plane = (1 - own) * (nl - 1)
        if e == 0:
            planes = [(metal.at[plane], plane_recv.at[0]), (start.at[plane], plane_recv.at[1])]
        else:
            planes = [(field.at[e - 1, plane, pl.ds(PAD, nr)], plane_recv.at[e + 1])]
        partner = (gx, gy, 1 - layer)
        return {
            "down": (gx < ngx - 1, copy(rows_send.at[e, 0], rows_recv.at[e, 0], 0, (lax.min(gx + 1, ngx - 1), gy, layer))),
            "up": (gx > 0, copy(rows_send.at[e, 1], rows_recv.at[e, 1], 1, (lax.max(gx - 1, 0), gy, layer))),
            "right": (gy < ngy - 1, copy(cols_send.at[e, pl.ds(0, 8)], cols_recv.at[e, 0], 2, (gx, lax.min(gy + 1, ngy - 1), layer))),
            "left": (gy > 0, copy(cols_send.at[e, pl.ds(8, 8)], cols_recv.at[e, 1], 3, (gx, lax.max(gy - 1, 0), layer))),
            "planes": [copy(s, d, 4 + i, partner) for i, (s, d) in enumerate(planes)],
        }

    def begin(e):
        ops = exchange(e)
        for op in ops["planes"]:
            op.start()
        for name in ("down", "up", "right", "left"):
            there, op = ops[name]

            @pl.when(there)
            def _():
                op.start()

    def finish(e):
        ops = exchange(e)
        arrives = {"down": gx > 0, "up": gx < ngx - 1, "right": gy > 0, "left": gy < ngy - 1}
        places = {
            "down": rows_recv.at[e, 0], "up": rows_recv.at[e, 1],
            "right": cols_recv.at[e, 0], "left": cols_recv.at[e, 1],
        }
        for name in ("down", "up", "right", "left"):
            there, op = ops[name]

            @pl.when(there)
            def _():
                op.wait_send()

            @pl.when(arrives[name])
            def _():
                op.wait_recv()

            @pl.when(jnp.logical_not(arrives[name]))
            def _():
                places[name][...] = jnp.zeros(places[name].shape, jnp.float32)
        for op in ops["planes"]:
            op.wait()
        halo = jnp.concatenate(
            [cols_recv[e, 0], cols_recv[e, 1], jnp.zeros((LANES - 16, nr), jnp.float32)], axis=0
        )
        col_halo[...] = jnp.transpose(halo)

    loads[1].wait()
    loads[2].wait()
    both = (metal, start)
    for l in range(2 * nl):
        ref = both[l // nl]
        rows_send[0, 0, pl.ds(l, 1), :] = ref[l % nl, pl.ds(nr - 1, 1), :]
        rows_send[0, 1, pl.ds(l, 1), :] = ref[l % nl, pl.ds(0, 1), :]
    packed = pack_columns(
        lambda l: both[l // nl][l % nl, :, pl.ds(0, LANES)][:, 0:1],
        lambda l: both[l // nl][l % nl, :, pl.ds(nc - LANES, LANES)][:, LANES - 1 :],
        2 * nl,
    )
    cols_send[0] = jnp.transpose(packed)[0:16]
    halves = nc // WIDE
    high = nr * halves
    acc[...] = jnp.zeros_like(acc)
    ids = lax.broadcasted_iota(jnp.int32, (max(high, WIDE), LANES), 0).astype(jnp.float32).astype(jnp.bfloat16)
    for k in (0, 5):
        loads[k].wait()
    live = count[0]
    wide_weight = jnp.concatenate(
        [jnp.broadcast_to(weight[k : k + 1], (16, weight.shape[1])) for k in range(weight.shape[0])], axis=1
    )
    nt = (((1,), (1,)), ((), ()))
    for i in range(chunks):
        if i == min(BARRIER_AT, chunks - 1):
            pl.semaphore_wait(barrier, total - 1)
            begin(0)
        chunk_loads[i].wait()

        amounts = lax.dot_general(wide_weight, pbuf[i], nt, preferred_element_type=jnp.float32)[0:1]
        position = i * slots + lax.broadcasted_iota(jnp.int32, (1, slots), 1)
        amounts = jnp.where(position < live, amounts, 0.0).astype(jnp.bfloat16)
        cell = cells[i]
        column = rem_by(cell, nc)
        tall = div_by(column, WIDE) * nr + div_by(cell, nc)
        tall = tall.astype(jnp.float32).astype(jnp.bfloat16)
        short = rem_by(column, WIDE).astype(jnp.float32).astype(jnp.bfloat16)
        left, right = [], []
        zero, one = jnp.zeros((), jnp.bfloat16), jnp.ones((), jnp.bfloat16)
        for g in range(slots // LANES):
            part = slice(g * LANES, (g + 1) * LANES)
            left.append(jnp.where(ids[:high] == tall[:, part], jnp.broadcast_to(amounts[:, part], (high, LANES)), zero))
            right.append(jnp.where(ids[:WIDE] == short[:, part], one, zero))
        acc[...] += lax.dot_general(
            jnp.concatenate(left, axis=1), jnp.concatenate(right, axis=1), nt,
            preferred_element_type=jnp.float32,
        )

    def current_copy():
        return pltpu.make_async_remote_copy(
            src_ref=acc, dst_ref=cur_recv, send_sem=send_sem.at[0, 6], recv_sem=recv_sem.at[0, 6],
            device_id=(gx, gy, 1 - layer), device_id_type=MESH,
        )

    current_copy().start()

    loads[3].wait()
    loads[4].wait()
    finish(0)
    lane_all = lax.broadcasted_iota(jnp.int32, (nr, nc), 1)
    row_all = lax.broadcasted_iota(jnp.int32, (nr, nc), 0)

    def beside(value, above, below, before, after):
        north_of = jnp.where(lane_all == nc - 1, after, pltpu.roll(value, nc - 1, 1))
        south_of = jnp.where(lane_all == 0, before, pltpu.roll(value, 1, 1))
        east_of = jnp.where(row_all == nr - 1, below, pltpu.roll(value, nr - 1, 0))
        west_of = jnp.where(row_all == 0, above, pltpu.roll(value, 1, 0))
        return east_of, west_of, north_of, south_of

    first = layer == 0
    for l in range(nl):
        value = metal[l]
        around = beside(
            value, rows_recv[0, 0, pl.ds(l, 1), :], rows_recv[0, 1, pl.ds(l, 1), :],
            col_halo[:, l : l + 1], col_halo[:, 8 + l : 9 + l],
        )
        links = [harmonic(value, other) for other in around]
        upper = metal[l + 1] if l + 1 < nl else jnp.where(first, plane_recv[0], 0.0)
        lower = metal[l - 1] if l else jnp.where(first, 0.0, plane_recv[0])
        links += [via[...] * harmonic(value, other) for other in (upper, lower)]
        whole = links[0] + links[1] + links[2] + links[3] + links[4] + links[5]
        if l + 1 == nl:
            whole = whole + jnp.where(first, 0.0, pad[...])
        diag[l] = whole
        inverse = 1.0 / whole
        dinv[l] = inverse
        for k in range(6):
            coef[k, l] = links[k] * inverse

    def inside(l, value, upper, lower):
        around = beside(value, 0.0, 0.0, 0.0, 0.0)
        out = coef[0, l] * around[0] + coef[1, l] * around[1] + coef[2, l] * around[2] + coef[3, l] * around[3]
        if upper is not None:
            out = out + coef[4, l] * upper
        if lower is not None:
            out = out + coef[5, l] * lower
        return out

    edge = (1 - layer) * (nl - 1)
    lane_west = lane == 0
    lane_east = lane == LANES - 1

    def across(f, shift, e, plane, weigh):
        odd = jnp.zeros((1, LANES), jnp.float32)

        def narrow(tile):
            wide = jnp.sum(tile, axis=0, keepdims=True)
            return functools.reduce(jnp.add, [wide[:, k : k + LANES] for k in range(0, wide.shape[1], LANES)])

        def add(l, rows, columns, first_row, term):
            odd = None
            field[f, l, pl.ds(PAD + first_row, rows), columns] += term
            if weigh is not None:
                heavy = diag[l, pl.ds(first_row, rows), columns] * field[weigh, l, pl.ds(PAD + first_row, rows), columns]
                odd = narrow(heavy * term)
            return odd

        parts = []
        everywhere = pl.ds(0, nc)
        for l in range(nl):
            parts.append(add(l, 1, everywhere, 0, coef[1, l, pl.ds(0, 1), :] * rows_recv[e, 0, pl.ds(shift + l, 1), :]))
            parts.append(add(l, 1, everywhere, nr - 1, coef[0, l, pl.ds(nr - 1, 1), :] * rows_recv[e, 1, pl.ds(shift + l, 1), :]))
            k = shift + l
            west, east = pl.ds(0, LANES), pl.ds(nc - LANES, LANES)
            parts.append(add(l, nr, west, 0, jnp.where(lane_west, coef[3, l, :, west] * col_halo[:, k : k + 1], 0.0)))
            parts.append(add(l, nr, east, 0, jnp.where(lane_east, coef[2, l, :, east] * col_halo[:, 8 + k : 9 + k], 0.0)))
        parts.append(add(edge, nr, everywhere, 0, coef[4 + layer, edge] * plane_recv[plane]))
        if weigh is not None:
            odd = functools.reduce(jnp.add, parts)
        return odd

    def send_field(e):
        f = e - 1
        for l in range(nl):
            rows_send[e, 0, pl.ds(l, 1), :] = field[f, l, pl.ds(PAD + nr - 1, 1), :]
            rows_send[e, 1, pl.ds(l, 1), :] = field[f, l, pl.ds(PAD, 1), :]
        packed = pack_columns(
            lambda l: field[f, l, pl.ds(PAD, nr), pl.ds(0, LANES)][:, 0:1],
            lambda l: field[f, l, pl.ds(PAD, nr), pl.ds(nc - LANES, LANES)][:, LANES - 1 :],
            nl,
        )
        cols_send[e] = jnp.transpose(packed)[0:16]
        begin(e)

    for l in range(nl):
        value = start[l]
        moved = inside(l, value, start[l + 1] if l + 1 < nl else None, start[l - 1] if l else None)
        field[0, l, pl.ds(PAD, nr), :] = moved - value
    across(0, nl, 0, 1, None)
    current_copy().wait()
    gathered = acc[...] + cur_recv[...]
    current = jnp.concatenate([gathered[h * nr : (h + 1) * nr] for h in range(halves)], axis=1)
    field[0, 0, pl.ds(PAD, nr), :] += jnp.where(first, dinv[0] * current, 0.0)

    tiles = []
    for e in range(1, ITERS + 1):
        f = e - 1
        send_field(e)
        even, odd = None, None
        for l in range(nl):
            value = field[f, l, pl.ds(PAD, nr), :]
            upper = field[f, l + 1, pl.ds(PAD, nr), :] if l + 1 < nl else None
            lower = field[f, l - 1, pl.ds(PAD, nr), :] if l else None
            moved = inside(l, value, upper, lower)
            field[e, l, pl.ds(PAD, nr), :] = moved
            heavy = diag[l] * value
            a = jnp.sum(heavy * value, axis=0, keepdims=True)
            b = jnp.sum(heavy * moved, axis=0, keepdims=True)
            even = a if even is None else even + a
            odd = b if odd is None else odd + b
        finish(e)
        more = across(e, 0, e, e + 1, f)
        tiles += [even, jnp.concatenate([odd[:, :LANES] + more, odd[:, LANES:]], axis=1)]

    row = lax.broadcasted_iota(jnp.int32, (1, LANES), 1)
    packed = jnp.zeros((1, LANES), jnp.float32)
    for j, tile in enumerate(tiles):
        packed = jnp.where(row == j, jnp.sum(tile, axis=1, keepdims=True), packed)
    sums[...] = packed
    gather[me] = packed

    peers(
        lambda device: pltpu.make_async_remote_copy(
            src_ref=sums, dst_ref=gather.at[me], send_sem=gsend, recv_sem=grecv,
            device_id=device, device_id_type=MESH,
        ).start()
    )
    most = gather.at[pl.ds(0, total - 1)]
    pltpu.make_async_copy(most, most, grecv).wait()
    pltpu.make_async_copy(most, most, gsend).wait()
    summed = jnp.sum(gather[...], axis=0)
    moments = [jnp.sum(jnp.where(row == j, summed, 0.0), axis=1, keepdims=True) for j in range(2 * ITERS)]
    moved, scaled = cg_coefficients(moments)
    for l in range(nl):
        parts = [field[c, l, pl.ds(PAD, nr), :] for c in range(ITERS + 1)]
        out = start[l]
        for c in range(ITERS):
            out = out + moved[c] * parts[c]
        drop[l] = out
        rest = scaled[0] * parts[0]
        for c in range(1, ITERS + 1):
            rest = rest + scaled[c] * parts[c]
        residual[l] = diag[l] * rest


def per_device(sizes, profiles, time_weight, slot_cell, inst_count, metal, via_density, pad, start_drop):
    nl, nr, nc = metal.shape
    inst, times = profiles.shape[-2:]
    slots = min(1024, inst)
    chunks = inst // slots
    total = sizes[0] * sizes[1] * sizes[2]
    vmem = pl.BlockSpec(memory_space=pltpu.VMEM)
    hbm = pl.BlockSpec(memory_space=pltpu.HBM)
    stay = functools.partial(pltpu.with_memory_space_constraint, memory_space=pltpu.HBM)
    high = nr * (nc // WIDE)
    f32 = jnp.float32
    out = jax.ShapeDtypeStruct((nl, nr, nc), f32)
    exchanges = ITERS + 1
    return pl.pallas_call(
        functools.partial(kernel, sizes, slots),
        out_shape=(out, out),
        in_specs=[
            hbm, hbm, hbm, vmem,
            hbm, hbm, hbm, hbm,
        ],
        out_specs=(vmem, vmem),
        scratch_shapes=[
            pltpu.VMEM((times // LANES, LANES), jnp.bfloat16),
            pltpu.VMEM((chunks, 1, slots), jnp.int32),
            pltpu.VMEM((nl, nr, nc), f32),
            pltpu.VMEM((nr, nc), f32),
            pltpu.VMEM((nr, nc), f32),
            pltpu.VMEM((nl, nr, nc), f32),
            pltpu.SemaphoreType.DMA((6,)),
            pltpu.VMEM((chunks, slots, times), jnp.bfloat16),
            pltpu.SemaphoreType.DMA((chunks,)),
            pltpu.VMEM((high, WIDE), f32),
            pltpu.VMEM((high, WIDE), f32),
            pltpu.VMEM((nl, nr, nc), f32),
            pltpu.VMEM((nl, nr, nc), f32),
            pltpu.VMEM((6, nl, nr, nc), f32),
            pltpu.VMEM((exchanges, nl, nr + 2 * PAD, nc), f32),
            pltpu.VMEM((exchanges, 2, 8, nc), f32),
            pltpu.VMEM((exchanges, 2, 8, nc), f32),
            pltpu.VMEM((nr, LANES), f32),
            pltpu.VMEM((exchanges, 16, nr), f32),
            pltpu.VMEM((exchanges, 2, 8, nr), f32),
            pltpu.VMEM((exchanges + 1, nr, nc), f32),
            pltpu.VMEM((nr, LANES), f32),
            pltpu.VMEM((1, LANES), f32),
            pltpu.VMEM((total, 1, LANES), f32),
            pltpu.SemaphoreType.DMA((exchanges, 7)),
            pltpu.SemaphoreType.DMA((exchanges, 7)),
            pltpu.SemaphoreType.DMA,
            pltpu.SemaphoreType.DMA,
        ],
        compiler_params=pltpu.CompilerParams(
            collective_id=0, has_side_effects=True, vmem_limit_bytes=40 * 1024 * 1024
        ),
    )(
        stay(profiles.reshape(chunks, slots, times)), stay(time_weight.reshape(times // LANES, LANES)),
        stay(slot_cell.reshape(chunks, 1, slots)), inst_count,
        stay(metal), stay(via_density), stay(pad), stay(start_drop),
    )


def solution(mesh):
    sizes = tuple(mesh.shape[axis] for axis in ("gx", "gy", "layer"))
    in_specs = (
        P("layer", "gx", "gy", None),
        P(),
        P("layer", "gx", "gy"),
        P("layer", "gx", "gy"),
        P("layer", "gx", "gy"),
        P("gx", "gy"),
        P("gx", "gy"),
        P("layer", "gx", "gy"),
    )
    out_specs = (P("layer", "gx", "gy"), P("layer", "gx", "gy"))
    return jax.shard_map(
        functools.partial(per_device, sizes), mesh=mesh, in_specs=in_specs, out_specs=out_specs, check_vma=False
    )
```

profile of v0, /device:TPU:0, one launch (start us, length us, event | category | flops | bytes accessed | tf_op | source)
XLA Modules:
  0.0 37.9 jit_solution(1805494070382596980)
XLA Ops:
  1.3 34.9 %shard_map.95 = (f32[3,128,512]{2,1,0:T(8,128)S(1)}, f32[3,128,512]{2,1,0:T(8,128)S(1)}) custom-call(bf16[16,1024,256]{2,1,0:T(8,128)(2,1)} %bitcast.3, bf16[2,128]{1,0:T(2,128)(2,1)} %bitcast.5, s32[16,1,1024]{2,1,0:T(1,128)} %bitcast.4, s32[1,1,1]{2,1,0:T(1,128)S(6)} %copy.12.count, f32[3,128,512]{2,1,0:T(8,128)} %metal_in.1, f32[128,512]{1,0:T(8,128)} %via_in.1, ...), custom_call_target="tpu_custom_call" | custom-call | tf_op jit(solution)/shard_map/pallas_call | solution.py:398
  36.2 0.9 %copy.13 = f32[3,128,512]{2,1,0:T(8,128)} copy(f32[3,128,512]{2,1,0:T(8,128)S(1)} %get-tuple-element.4) | data formatting | bytes 1572864
  37.0 0.9 %copy.14 = f32[3,128,512]{2,1,0:T(8,128)} copy(f32[3,128,512]{2,1,0:T(8,128)S(1)} %get-tuple-element.5) | data formatting | bytes 1572864
where the time goes:
time: 38.1 us; the launch traced here: 37.9 us
  Pallas kernels  34.9 us (92%)
  local copies, waits for them, and re-layouts  1.76 us (5%)
  between operations  1.29 us (3%)
    pallas_call x1, Pallas kernels, per_device(): pl.pallas_call(functools.partial(kernel, sizes, slots), out_shape=(out, o...  34.9 us
    unnamed x2, local copies, waits for them, and re-layouts  1.76 us

commit v1 on v0

v1 whole, which is shorter than its diff:
```python
import functools

import jax
import jax.numpy as jnp
from jax import lax
from jax.experimental import pallas as pl
from jax.experimental.pallas import tpu as pltpu
from jax.sharding import PartitionSpec as P

ITERS = 3
LANES = 128
SUB = 8
WIDE = 256
TINY = 5e-31
BARRIER_AT = 6
MESH = pl.DeviceIdType.MESH


def div_by(values, size):
    if size & (size - 1) == 0:
        return lax.shift_right_logical(values, jnp.full_like(values, size.bit_length() - 1))
    return lax.div(values, size)


def rem_by(values, size):
    return values & (size - 1) if size & (size - 1) == 0 else lax.rem(values, size)


def cg_coefficients(moments):
    def form(left, right):
        total = None
        for a, x in enumerate(left):
            for b, y in enumerate(right):
                term = x * y * moments[a + b]
                total = term if total is None else total + term
        return total

    one = jnp.ones_like(moments[0])
    scaled, direction = [one], [one]
    moved = [jnp.zeros_like(one)] * ITERS
    energy = form(scaled, scaled)
    for iteration in range(ITERS):
        image = [
            (direction[c] if c < len(direction) else 0.0) - (direction[c - 1] if c else 0.0)
            for c in range(len(direction) + 1)
        ]
        step = energy / form(direction, image)
        for c, value in enumerate(direction):
            moved[c] = moved[c] + step * value
        scaled = [
            (scaled[c] if c < len(scaled) else 0.0) - step * image[c] for c in range(len(image))
        ]
        if iteration + 1 < ITERS:
            energy_next = form(scaled, scaled)
            momentum = energy_next / energy
            direction = [
                scaled[c] + (momentum * direction[c] if c < len(direction) else 0.0)
                for c in range(len(scaled))
            ]
            energy = energy_next
    return moved, scaled


def kernel(
    sizes, slots, profiles, weight_in, cells_in, count, metal_in, via_in, pad_in, start_in, drop, residual,
    weight, cells, pbuf, psem, isem,
    raw, edge, inner, row_src, col_src, row_pack, col_pack, row_recv, col_recv, corner_recv,
    acc, strips, cur_recv, cur_row, cur_col, cur_corner, col_turn, cur,
    rows_link, cols_link, up_link, dinv, field, grad, away, away_dinv, away_start,
    sums, gather, send_sem, recv_sem, part_send, part_recv, back_send, back_recv, gsend, grecv,
):
    ngx, ngy, nlayer = sizes
    total = ngx * ngy * nlayer
    nl, nr, nc = metal_in.shape
    nz = nlayer * nl
    half = nr // nlayer
    ext = half + SUB
    high = ext // SUB
    flat = nc // LANES
    tiles = flat + 1
    halves = nc // WIDE
    gx, gy, layer = lax.axis_index("gx"), lax.axis_index("gy"), lax.axis_index("layer")
    me = (gx * ngy + gy) * nlayer + layer
    chunks = pbuf.shape[0]
    first = layer == 0
    mine = layer * nl
    theirs = (1 - layer) * nl
    own_row = layer * half
    other_row = (1 - layer) * half
    own_inner = half - SUB * layer
    other_inner = half - SUB * (1 - layer)

    def coords(number):
        return (number // (ngy * nlayer), (number // nlayer) % ngy, number % nlayer)

    loads = []

    def load(src, dst):
        op = pltpu.make_async_copy(src, dst, isem.at[len(loads)])
        loads.append(op)
        return op

    def edges(ref, at):
        cut = ref.at[:, pl.ds(0, SUB)], ref.at[:, pl.ds(nr - SUB, SUB)]
        side = ref.at[:, :, pl.ds(0, LANES)], ref.at[:, :, pl.ds(nc - LANES, LANES)]
        return [load(cut[d], row_src.at[d, pl.ds(at, nl)]) for d in (0, 1)] + [
            load(side[d], col_src.at[d, pl.ds(at, nl)]) for d in (0, 1)
        ]

    def flat_edges(ref, at):
        cut = ref.at[pl.ds(0, SUB)], ref.at[pl.ds(nr - SUB, SUB)]
        side = ref.at[:, pl.ds(0, LANES)], ref.at[:, pl.ds(nc - LANES, LANES)]
        return [load(cut[d], row_src.at[d, at]) for d in (0, 1)] + [load(side[d], col_src.at[d, at]) for d in (0, 1)]

    edge_loads = edges(metal_in, 0) + edges(start_in, nl) + flat_edges(via_in, 2 * nl) + flat_edges(pad_in, 2 * nl + 1)
    slot_loads = [load(weight_in, weight), load(cells_in, cells)]
    own_loads = []
    for k, ref in enumerate((metal_in, start_in)):
        own_loads.append(load(ref.at[:, pl.ds(own_row, half)], raw.at[pl.ds(k * nz + mine, nl), pl.ds(0, half)]))
        own_loads.append(load(ref.at[:, pl.ds(own_inner, SUB)], inner.at[pl.ds(k * nz + mine, nl)]))
    for k, ref in enumerate((via_in, pad_in)):
        own_loads.append(load(ref.at[pl.ds(own_row, half)], raw.at[2 * nz + k, pl.ds(0, half)]))
        own_loads.append(load(ref.at[pl.ds(own_inner, SUB)], inner.at[2 * nz + k]))
    own_loads.append(load(start_in.at[:, pl.ds(other_row, half)], away_start))
    chunk_loads = [pltpu.make_async_copy(profiles.at[i], pbuf.at[i], psem.at[i]) for i in range(chunks)]
    for op in edge_loads + slot_loads + chunk_loads + own_loads:
        op.start()

    barrier = pltpu.get_barrier_semaphore()

    def other(at, offset, size):
        return at ^ offset if size & (size - 1) == 0 else lax.rem(at + offset, size)

    def peers(visit):
        if total <= 64:
            offsets = [(a, b, c) for a in range(ngx) for b in range(ngy) for c in range(nlayer)]
            for a, b, c in sorted(offsets[1:], key=lambda o: -(o[0].bit_count() + o[1] + 0.5 * o[2])):
                visit((other(gx, a, ngx), other(gy, b, ngy), other(layer, c, nlayer)))
        else:
            def one(k, carry):
                visit(coords(lax.rem(me + k, total)))
                return carry

            lax.fori_loop(1, total, one, 0)

    peers(lambda device: pl.semaphore_signal(barrier, inc=1, device_id=device, device_id_type=MESH))

    above, below, before, after = gx > 0, gx < ngx - 1, gy > 0, gy < ngy - 1
    gx_up, gx_down = lax.max(gx - 1, 0), lax.min(gx + 1, ngx - 1)
    gy_left, gy_right = lax.max(gy - 1, 0), lax.min(gy + 1, ngy - 1)
    outside = jnp.logical_or(jnp.logical_and(first, above), jnp.logical_and(jnp.logical_not(first), below))
    RIGHT, LEFT = 0, 1

    def exchange(stage, row_of, col_of, corner_of, row_to, col_to, corner_to):
        both = jnp.logical_and
        plan = [
            (above, (gx_up, gy, 1), row_of(0), row_to.at[layer], layer),
            (below, (gx_down, gy, 0), row_of(1), row_to.at[layer], layer),
        ]
        for there, at, side, edge_at in ((before, gy_left, RIGHT, 0), (after, gy_right, LEFT, 1)):
            for part in range(nlayer):
                plan.append((there, (gx, at, part), col_of(edge_at, part), col_to.at[side, layer], 2 + 2 * side + layer))
            plan.append((both(above, there), (gx_up, at, 1), corner_of(0, edge_at), corner_to.at[side, layer], 6 + 2 * side + layer))
            plan.append((both(below, there), (gx_down, at, 0), corner_of(1, edge_at), corner_to.at[side, layer], 6 + 2 * side + layer))
        sends = [
            (
                there,
                pltpu.make_async_remote_copy(
                    src_ref=src, dst_ref=dst, send_sem=send_sem.at[stage, k], recv_sem=recv_sem.at[stage, r],
                    device_id=device, device_id_type=MESH,
                ),
            )
            for k, (there, device, src, dst, r) in enumerate(plan)
        ]
        arrivals = [(outside, row_to, 0)]
        for there, side in ((after, RIGHT), (before, LEFT)):
            arrivals.append((there, col_to.at[side], 2 + 2 * side))
            arrivals.append((both(outside, there), corner_to.at[side], 6 + 2 * side))
        return sends, arrivals

    def begin(sends):
        for there, op in sends:
            @pl.when(there)
            def _():
                op.start()

    def sent(sends):
        for there, op in sends:
            @pl.when(there)
            def _():
                op.wait_send()

    def receive(stage, arrivals, blank):
        for there, place, at in arrivals:
            @pl.when(there)
            def _():
                for k in range(nlayer):
                    pltpu.make_async_copy(place.at[k], place.at[k], recv_sem.at[stage, at + k]).wait()

            @pl.when(jnp.logical_not(there))
            def _():
                place[...] = jnp.full(place.shape, blank, jnp.float32)

    partner = (gx, gy, 1 - layer)

    def to_partner(src, dst, send, recv):
        return pltpu.make_async_remote_copy(
            src_ref=src, dst_ref=dst, send_sem=send, recv_sem=recv, device_id=partner, device_id_type=MESH
        )

    window = [pl.ds(k * (half - SUB), ext) for k in range(nlayer)]
    halo_sends, halo_arrivals = exchange(
        0,
        lambda d: row_pack.at[d],
        lambda d, part: col_pack.at[window[part]],
        lambda r, d: col_pack.at[pl.ds((nr - SUB) * r, SUB)],
        row_recv, col_recv, corner_recv,
    )
    plane_sends = []
    for k, ref in enumerate((metal_in, start_in)):
        at = pl.ds(k * nz + mine, nl)
        for src, dst in (
            (ref.at[:, pl.ds(other_row, half)], raw.at[at, pl.ds(0, half)]),
            (ref.at[:, pl.ds(other_inner, SUB)], inner.at[at]),
        ):
            n = len(plane_sends)
            plane_sends.append(to_partner(src, dst, part_send.at[n], part_recv.at[n]))

    for op in edge_loads:
        op.wait()
    sub = lax.broadcasted_iota(jnp.int32, (SUB, nc), 0)
    pairs = [(l, nl + l) for l in range(nl)] + [(2 * nl, 2 * nl + 1)]
    for k, (a, b) in enumerate(pairs):
        low = pltpu.roll(row_src[0, b], SUB // 2, 0)
        row_pack[0, k] = jnp.where(sub < SUB // 2, row_src[0, a], low)
        low = pltpu.roll(row_src[1, b], SUB // 2, 0)
        row_pack[1, k] = jnp.where(sub < SUB // 2, low, row_src[1, a])
    lane = lax.broadcasted_iota(jnp.int32, (nr, LANES), 1)
    kinds = 2 * nl + 2
    owner = ((lane + 4) >> 3) & (LANES // 8 - 1)
    packed = jnp.ones((nr, LANES), jnp.float32)
    for q in range(kinds):
        pair = jnp.where(lane < LANES // 2, col_src[0, q], col_src[1, q])
        if q:
            pair = pltpu.roll(pair, 8 * q, 1)
        packed = jnp.where(owner == q, pair, packed)
    col_pack[...] = packed

    tall_size = nr * halves
    acc[...] = jnp.zeros_like(acc)
    ids = lax.broadcasted_iota(jnp.int32, (max(tall_size, WIDE), LANES), 0).astype(jnp.float32).astype(jnp.bfloat16)
    for op in slot_loads:
        op.wait()
    live = count[0]
    wide_weight = jnp.concatenate(
        [jnp.broadcast_to(weight[k : k + 1], (16, weight.shape[1])) for k in range(weight.shape[0])], axis=1
    )
    nt = (((1,), (1,)), ((), ()))
    for i in range(chunks):
        if i == min(BARRIER_AT, chunks - 1):
            pl.semaphore_wait(barrier, total - 1)
            begin(halo_sends)
            for op in plane_sends:
                op.start()
        chunk_loads[i].wait()
        amounts = lax.dot_general(wide_weight, pbuf[i], nt, preferred_element_type=jnp.float32)[0:1]
        position = i * slots + lax.broadcasted_iota(jnp.int32, (1, slots), 1)
        amounts = jnp.where(position < live, amounts, 0.0).astype(jnp.bfloat16)
        cell = cells[i]
        column = rem_by(cell, nc)
        tall = div_by(column, WIDE) * nr + div_by(cell, nc)
        tall = tall.astype(jnp.float32).astype(jnp.bfloat16)
        short = rem_by(column, WIDE).astype(jnp.float32).astype(jnp.bfloat16)
        left, right = [], []
        zero, one = jnp.zeros((), jnp.bfloat16), jnp.ones((), jnp.bfloat16)
        for g in range(slots // LANES):
            part = slice(g * LANES, (g + 1) * LANES)
            left.append(jnp.where(ids[:tall_size] == tall[:, part], jnp.broadcast_to(amounts[:, part], (tall_size, LANES)), zero))
            right.append(jnp.where(ids[:WIDE] == short[:, part], one, zero))
        acc[...] += lax.dot_general(
            jnp.concatenate(left, axis=1), jnp.concatenate(right, axis=1), nt,
            preferred_element_type=jnp.float32,
        ).reshape(acc.shape)

    strips[0] = jnp.transpose(acc[0, :, pl.ds(0, LANES)])[0:SUB]
    strips[1] = jnp.transpose(acc[halves - 1, :, pl.ds(WIDE - LANES, LANES)])[LANES - SUB :]
    corner_tiles = ((0, pl.ds(0, LANES)), (halves - 1, pl.ds(WIDE - LANES, LANES)))
    cur_sends, cur_arrivals = exchange(
        1,
        lambda d: acc.at[:, pl.ds((nr - SUB) * d, SUB)],
        lambda d, part: strips.at[d],
        lambda r, d: acc.at[corner_tiles[d][0], pl.ds((nr - SUB) * r, SUB), corner_tiles[d][1]],
        cur_row, cur_col, cur_corner,
    )
    n = len(plane_sends)
    cur_op = to_partner(
        acc.at[:, pl.ds((1 - layer) * (half - SUB), ext)], cur_recv, part_send.at[n], part_recv.at[n]
    )
    begin(cur_sends)
    cur_op.start()

    for op in own_loads:
        op.wait()
    for op in plane_sends:
        op.wait()
    receive(0, halo_arrivals, TINY)
    inward = (sub < SUB // 2) == first
    for k in range(nlayer):
        for l in range(nl):
            got = row_recv[k, l]
            for q, value in ((k * nl + l, got), (nz + k * nl + l, pltpu.roll(got, SUB // 2, 0))):
                raw[q, pl.ds(half, SUB)] = jnp.where(inward, inner[q], value)
    got = row_recv[0, nl]
    for q, value in ((2 * nz, got), (2 * nz + 1, pltpu.roll(got, SUB // 2, 0))):
        raw[q, pl.ds(half, SUB)] = jnp.where(inward, inner[q], value)
    lane_half = lane[:half]
    lane_sub = lane[:SUB]
    inward_tile = inward[:, :LANES]
    lane_ext = lax.broadcasted_iota(jnp.int32, (ext, LANES), 1)
    rim = jnp.logical_or(lane_ext < 4, lane_ext >= LANES - 4)
    body_at = pl.ds(pl.multiple_of(SUB * layer, SUB), half)
    inner_at = pl.ds(pl.multiple_of(half * (1 - layer), SUB), SUB)
    for k in range(nlayer):
        def side_of(tall, cut, corner):
            return jnp.where((cut & 7) < 4, tall[0], tall[1])

        main = jnp.where((lane_half & 7) < 4, col_recv[RIGHT, k, body_at], col_recv[LEFT, k, body_at])
        near = jnp.where((lane_sub & 7) < 4, col_recv[RIGHT, k, inner_at], col_recv[LEFT, k, inner_at])
        far = jnp.where((lane_sub & 7) < 4, corner_recv[RIGHT, k], corner_recv[LEFT, k])
        mixed = jnp.concatenate([main, jnp.where(inward_tile, near, far)], axis=0)
        spots = [(q, k * nl + q) for q in range(nl)] + [(nl + q, nz + k * nl + q) for q in range(nl)]
        if k == 0:
            spots += [(2 * nl, 2 * nz), (2 * nl + 1, 2 * nz + 1)]
        for q, plane in spots:
            turned = pltpu.roll(mixed, LANES - 8 * q, 1) if q else mixed
            edge[plane] = jnp.where(rim, turned, 1.0)

    shape = (tiles, high, SUB, LANES)
    sub_at = lax.broadcasted_iota(jnp.int32, shape, 2)
    lane_at = lax.broadcasted_iota(jnp.int32, shape, 3)
    last_sub, first_sub = sub_at == SUB - 1, sub_at == 0
    last_lane, first_lane = lane_at == LANES - 1, lane_at == 0

    def plane_of(q):
        value = raw[q]
        parts = [value[:, t * LANES : (t + 1) * LANES] for t in range(flat)] + [edge[q]]
        return jnp.stack([part.reshape(high, SUB, LANES) for part in parts])

    def keep(ref, at, value):
        ref[at] = value.reshape(tiles, ext, LANES)

    def held(ref, at):
        return ref[at].reshape(shape)

    def row_up(x):
        y = pltpu.roll(x.reshape(tiles * high, SUB, LANES), SUB - 1, 1).reshape(shape)
        return jnp.where(last_sub, jnp.concatenate([y[:, 1:], y[:, :1]], axis=1), y)

    def row_down(x):
        y = pltpu.roll(x.reshape(tiles * high, SUB, LANES), 1, 1).reshape(shape)
        return jnp.where(first_sub, jnp.concatenate([y[:, -1:], y[:, :-1]], axis=1), y)

    def lane_up(x):
        y = pltpu.roll(x.reshape(tiles * ext, LANES), LANES - 1, 1).reshape(shape)
        return jnp.where(last_lane, jnp.concatenate([y[1:], y[:1]], axis=0), y)

    def lane_down(x):
        y = pltpu.roll(x.reshape(tiles * ext, LANES), 1, 1).reshape(shape)
        return jnp.where(first_lane, jnp.concatenate([y[-1:], y[:-1]], axis=0), y)

    def pull(z, value, upper, lower):
        rows, cols = held(rows_link, z), held(cols_link, z)
        out = rows * row_up(value) + row_down(rows * value) + cols * lane_up(value) + lane_down(cols * value)
        if upper is not None:
            out = out + held(up_link, z) * upper
        if lower is not None:
            out = out + held(up_link, z - 1) * lower
        return out

    moments = [None] * (2 * ITERS)

    def measure(j, left, right):
        own = (left * right)[:flat, : half // SUB]
        value = jnp.sum(own.reshape(flat * (half // SUB), SUB, LANES), axis=0)
        moments[j] = value if moments[j] is None else moments[j] + value

    via = plane_of(2 * nz)
    resist = 0.5 / plane_of(0)
    for z in range(nz):
        keep(rows_link, z, 1.0 / (resist + row_up(resist)))
        keep(cols_link, z, 1.0 / (resist + lane_up(resist)))
        if z + 1 < nz:
            upper = 0.5 / plane_of(z + 1)
            keep(up_link, z, via / (resist + upper))
            resist = upper
    for z in range(nz):
        rows, cols = held(rows_link, z), held(cols_link, z)
        whole = rows + row_down(rows) + cols + lane_down(cols)
        if z + 1 < nz:
            whole = whole + held(up_link, z)
        if z:
            whole = whole + held(up_link, z - 1)
        if z + 1 == nz:
            whole = whole + plane_of(2 * nz + 1)
        inverse = 1.0 / whole
        keep(dinv, z, inverse)
        value = plane_of(nz + z)
        image = pull(z, value, plane_of(nz + z + 1) if z + 1 < nz else None, plane_of(nz + z - 1) if z else None)
        image = image - whole * value
        keep(grad.at[0], z, image)
        if z:
            scaled = inverse * image
            keep(field.at[0], z, scaled)
            measure(0, scaled, image)

    back = [
        to_partner(src.at[pl.ds(theirs, nl), pl.ds(0, flat), pl.ds(0, half)], dst, back_send.at[k], back_recv.at[k])
        for k, (src, dst) in enumerate([(grad.at[c], away.at[c]) for c in range(ITERS + 1)] + [(dinv, away_dinv)])
    ]
    back[ITERS + 1].start()

    def advance(c, z):
        source = field.at[c - 1]
        value = held(source, z)
        image = pull(z, value, held(source, z + 1) if z + 1 < nz else None, held(source, z - 1) if z else None)
        keep(grad.at[c], z, image)
        measure(2 * c - 1, value, image)
        if c < ITERS:
            scaled = held(dinv, z) * image
            keep(field.at[c], z, scaled)
            measure(2 * c, scaled, image)

    for c in range(1, ITERS + 1):
        for z in range(c + 1, nz):
            advance(c, z)

    cur_op.wait()
    receive(1, cur_arrivals, 0.0)
    whole_row = pl.ds(pl.multiple_of(own_row, SUB), half)
    inner_row = pl.ds(pl.multiple_of(own_inner, SUB), SUB)
    turned = jnp.concatenate(
        [
            cur_col[RIGHT, 0] + cur_col[RIGHT, 1],
            jnp.zeros((LANES - 2 * SUB, nr), jnp.float32),
            cur_col[LEFT, 0] + cur_col[LEFT, 1],
        ],
        axis=0,
    )
    col_turn[...] = jnp.transpose(turned)
    for t in range(tiles):
        if t < flat:
            h, at = t // (WIDE // LANES), pl.ds(t % (WIDE // LANES) * LANES, LANES)
            main = acc[h, whole_row, at] + cur_recv[h, body_at, at]
            near = acc[h, inner_row, at] + cur_recv[h, inner_at, at]
            far = cur_row[0, h, :, at] + cur_row[1, h, :, at]
        else:
            main = col_turn[whole_row]
            near = col_turn[inner_row]
            far = jnp.where(
                lane_sub < LANES // 2, cur_corner[RIGHT, 0] + cur_corner[RIGHT, 1], cur_corner[LEFT, 0] + cur_corner[LEFT, 1]
            )
        cur[t, pl.ds(0, half)] = main
        cur[t, pl.ds(half, SUB)] = jnp.where(inward_tile, near, far)
    image = held(grad.at[0], 0) + cur[...].reshape(shape)
    keep(grad.at[0], 0, image)
    scaled = held(dinv, 0) * image
    keep(field.at[0], 0, scaled)
    measure(0, scaled, image)
    back[0].start()
    for c in range(1, ITERS + 1):
        for z in range(min(c + 1, nz)):
            advance(c, z)
        back[c].start()

    row = lax.broadcasted_iota(jnp.int32, (1, LANES), 1)
    packed = jnp.zeros((1, LANES), jnp.float32)
    for j, tile in enumerate(moments):
        one_row = jnp.sum(tile, axis=0, keepdims=True)
        packed = jnp.where(row == j, jnp.sum(one_row, axis=1, keepdims=True), packed)
    sums[...] = packed
    gather[me] = packed
    peers(
        lambda device: pltpu.make_async_remote_copy(
            src_ref=sums, dst_ref=gather.at[me], send_sem=gsend, recv_sem=grecv,
            device_id=device, device_id_type=MESH,
        ).start()
    )
    for op in back:
        op.wait()
    sent(halo_sends)
    sent(cur_sends)
    most = gather.at[pl.ds(0, total - 1)]
    pltpu.make_async_copy(most, most, grecv).wait()
    pltpu.make_async_copy(most, most, gsend).wait()
    summed = jnp.sum(gather[...], axis=0)
    totals = [jnp.sum(jnp.where(row == j, summed, 0.0), axis=1, keepdims=True) for j in range(2 * ITERS)]
    moved, scaled = cg_coefficients(totals)
    own_out = pl.ds(pl.multiple_of(own_row, SUB), half)
    other_out = pl.ds(pl.multiple_of(other_row, SUB), half)
    for l in range(nl):
        for t in range(flat):
            at = pl.ds(t * LANES, LANES)
            own = pl.ds(0, half)
            for place, parts, inverse, start in (
                (own_out, [grad[c, mine + l, t, own] for c in range(ITERS + 1)], dinv[mine + l, t, own], raw[nz + mine + l, own, at]),
                (other_out, [away[c, l, t] for c in range(ITERS + 1)], away_dinv[l, t], away_start[l, :, at]),
            ):
                step = moved[0] * parts[0]
                for c in range(1, ITERS):
                    step = step + moved[c] * parts[c]
                drop[l, place, at] = start + inverse * step
                rest = scaled[0] * parts[0]
                for c in range(1, ITERS + 1):
                    rest = rest + scaled[c] * parts[c]
                residual[l, place, at] = rest


def per_device(sizes, profiles, time_weight, slot_cell, inst_count, metal, via_density, pad, start_drop):
    nl, nr, nc = metal.shape
    inst, times = profiles.shape[-2:]
    slots = min(1024, inst)
    chunks = inst // slots
    total = sizes[0] * sizes[1] * sizes[2]
    nlayer = sizes[2]
    nz, half = nl * nlayer, nr // nlayer
    ext, tiles, halves = half + SUB, nc // LANES + 1, nc // WIDE
    kinds, pairs, count = 2 * nl + 2, nl + 1, ITERS + 1
    vmem = pl.BlockSpec(memory_space=pltpu.VMEM)
    hbm = pl.BlockSpec(memory_space=pltpu.HBM)
    stay = functools.partial(pltpu.with_memory_space_constraint, memory_space=pltpu.HBM)
    out = jax.ShapeDtypeStruct((nl, nr, nc), jnp.float32)

    def room(*shape):
        return pltpu.VMEM(shape, jnp.float32)

    DMA = pltpu.SemaphoreType.DMA
    return pl.pallas_call(
        functools.partial(kernel, sizes, slots),
        out_shape=(out, out),
        in_specs=[hbm, hbm, hbm, vmem, hbm, hbm, hbm, hbm],
        out_specs=(vmem, vmem),
        scratch_shapes=[
            pltpu.VMEM((times // LANES, LANES), jnp.bfloat16),
            pltpu.VMEM((chunks, 1, slots), jnp.int32),
            pltpu.VMEM((chunks, slots, times), jnp.bfloat16),
            DMA((chunks,)),
            DMA((27,)),
            room(2 * nz + 2, ext, nc),
            room(2 * nz + 2, ext, LANES),
            room(2 * nz + 2, SUB, nc),
            room(2, kinds, SUB, nc),
            room(2, kinds, nr, LANES),
            room(2, pairs, SUB, nc),
            room(nr, LANES),
            room(nlayer, pairs, SUB, nc),
            room(2, nlayer, ext, LANES),
            room(2, nlayer, SUB, LANES),
            room(halves, nr, WIDE),
            room(2, SUB, nr),
            room(halves, ext, WIDE),
            room(nlayer, halves, SUB, WIDE),
            room(2, nlayer, SUB, nr),
            room(2, nlayer, SUB, LANES),
            room(nr, LANES),
            room(tiles, ext, LANES),
            room(nz, tiles, ext, LANES),
            room(nz, tiles, ext, LANES),
            room(nz - 1, tiles, ext, LANES),
            room(nz, tiles, ext, LANES),
            room(ITERS, nz, tiles, ext, LANES),
            room(count, nz, tiles, ext, LANES),
            room(count, nl, tiles - 1, half, LANES),
            room(nl, tiles - 1, half, LANES),
            room(nl, half, nc),
            room(1, LANES),
            room(total, 1, LANES),
            DMA((2, 10)),
            DMA((2, 10)),
            DMA((5,)),
            DMA((5,)),
            DMA((count + 1,)),
            DMA((count + 1,)),
            DMA,
            DMA,
        ],
        compiler_params=pltpu.CompilerParams(
            collective_id=0, has_side_effects=True, vmem_limit_bytes=48 * 1024 * 1024
        ),
    )(
        stay(profiles.reshape(chunks, slots, times)), stay(time_weight.reshape(times // LANES, LANES)),
        stay(slot_cell.reshape(chunks, 1, slots)), inst_count,
        stay(metal), stay(via_density), stay(pad), stay(start_drop),
    )


def solution(mesh):
    sizes = tuple(mesh.shape[axis] for axis in ("gx", "gy", "layer"))
    in_specs = (
        P("layer", "gx", "gy", None),
        P(),
        P("layer", "gx", "gy"),
        P("layer", "gx", "gy"),
        P("layer", "gx", "gy"),
        P("gx", "gy"),
        P("gx", "gy"),
        P("layer", "gx", "gy"),
    )
    out_specs = (P("layer", "gx", "gy"), P("layer", "gx", "gy"))
    return jax.shard_map(
        functools.partial(per_device, sizes), mesh=mesh, in_specs=in_specs, out_specs=out_specs, check_vma=False
    )
```

time: 38.1 us -> 28.6 us (0.75)
  Pallas kernels: 34.9 us -> 25.4 us
    pallas_call x1, Pallas kernels: 34.9 us -> 25.4 us  [per_device(): pl.pallas_call(functools.partial(kernel, sizes, slots), out_shape=(out, o...]
where the time goes in v1:
time: 28.6 us; the launch traced here: 28.5 us
  Pallas kernels  25.4 us (89%)
  local copies, waits for them, and re-layouts  1.76 us (6%)
  between operations  1.29 us (5%)
    pallas_call x1, Pallas kernels, per_device(): pl.pallas_call(functools.partial(kernel, sizes, slots), out_shape=(out, o...  25.4 us
    unnamed x2, local copies, waits for them, and re-layouts  1.76 us

profile of v1, /device:TPU:0, one launch (start us, length us, event | category | flops | bytes accessed | tf_op | source)
XLA Modules:
  0.0 28.5 jit_solution(11622926999170302552)
XLA Ops:
  1.3 25.4 %shard_map.95 = (f32[3,128,512]{2,1,0:T(8,128)S(1)}, f32[3,128,512]{2,1,0:T(8,128)S(1)}) custom-call(bf16[16,1024,256]{2,1,0:T(8,128)(2,1)} %bitcast.3, bf16[2,128]{1,0:T(2,128)(2,1)} %bitcast.5, s32[16,1,1024]{2,1,0:T(1,128)} %bitcast.4, s32[1,1,1]{2,1,0:T(1,128)S(6)} %copy.12.count, f32[3,128,512]{2,1,0:T(8,128)} %metal_in.1, f32[128,512]{1,0:T(8,128)} %via_in.1, ...), custom_call_target="tpu_custom_call" | custom-call | tf_op jit(solution)/shard_map/pallas_call | solution.py:537
  26.7 0.9 %copy.13 = f32[3,128,512]{2,1,0:T(8,128)} copy(f32[3,128,512]{2,1,0:T(8,128)S(1)} %get-tuple-element.4) | data formatting | bytes 1572864
  27.6 0.9 %copy.14 = f32[3,128,512]{2,1,0:T(8,128)} copy(f32[3,128,512]{2,1,0:T(8,128)S(1)} %get-tuple-element.5) | data formatting | bytes 1572864

commit v2 on v1

--- a/solution.py
+++ b/solution.py
@@ -12,7 +12,8 @@
 SUB = 8
 WIDE = 256
 TINY = 5e-31
-BARRIER_AT = 6
+SEND_AT = 1
+PARTS = 2
 MESH = pl.DeviceIdType.MESH
 
 
@@ -64,10 +65,10 @@
 def kernel(
     sizes, slots, profiles, weight_in, cells_in, count, metal_in, via_in, pad_in, start_in, drop, residual,
     weight, cells, pbuf, psem, isem,
-    raw, edge, inner, row_src, col_src, row_pack, col_pack, row_recv, col_recv, corner_recv,
-    acc, strips, cur_recv, cur_row, cur_col, cur_corner, col_turn, cur,
-    rows_link, cols_link, up_link, dinv, field, grad, away, away_dinv, away_start,
-    sums, gather, send_sem, recv_sem, part_send, part_recv, back_send, back_recv, gsend, grecv,
+    raw, inner, row_src, col_src, row_pack, col_pack, row_recv, col_recv, corner_recv,
+    acc_parts, acc, strips, cur_recv, cur_row, cur_col, cur_corner, col_turn, cur,
+    began, rows_link, cols_link, up_link, dinv, field, grad, away, away_dinv, away_start,
+    sums, gather, send_sem, recv_sem, part_send, part_recv, back_send, back_recv, gsend, grecv, ready,
 ):
     ngx, ngy, nlayer = sizes
     total = ngx * ngy * nlayer
@@ -115,15 +116,19 @@
     edge_loads = edges(metal_in, 0) + edges(start_in, nl) + flat_edges(via_in, 2 * nl) + flat_edges(pad_in, 2 * nl + 1)
     slot_loads = [load(weight_in, weight), load(cells_in, cells)]
     own_loads = []
+    lanes_of = [pl.ds(t * LANES, LANES) for t in range(flat)]
     for k, ref in enumerate((metal_in, start_in)):
-        own_loads.append(load(ref.at[:, pl.ds(own_row, half)], raw.at[pl.ds(k * nz + mine, nl), pl.ds(0, half)]))
+        for t, at in enumerate(lanes_of):
+            own_loads.append(load(ref.at[:, pl.ds(own_row, half), at], raw.at[pl.ds(k * nz + mine, nl), t, pl.ds(0, half)]))
         own_loads.append(load(ref.at[:, pl.ds(own_inner, SUB)], inner.at[pl.ds(k * nz + mine, nl)]))
     for k, ref in enumerate((via_in, pad_in)):
-        own_loads.append(load(ref.at[pl.ds(own_row, half)], raw.at[2 * nz + k, pl.ds(0, half)]))
+        for t, at in enumerate(lanes_of):
+            own_loads.append(load(ref.at[pl.ds(own_row, half), at], raw.at[2 * nz + k, t, pl.ds(0, half)]))
         own_loads.append(load(ref.at[pl.ds(own_inner, SUB)], inner.at[2 * nz + k]))
-    own_loads.append(load(start_in.at[:, pl.ds(other_row, half)], away_start))
+    for t, at in enumerate(lanes_of):
+        own_loads.append(load(start_in.at[:, pl.ds(other_row, half), at], away_start.at[:, t, pl.ds(0, half)]))
     chunk_loads = [pltpu.make_async_copy(profiles.at[i], pbuf.at[i], psem.at[i]) for i in range(chunks)]
-    for op in edge_loads + slot_loads + chunk_loads + own_loads:
+    for op in slot_loads + chunk_loads[:2] + edge_loads + chunk_loads[2:] + own_loads:
         op.start()
 
     barrier = pltpu.get_barrier_semaphore()
@@ -143,7 +148,32 @@
 
             lax.fori_loop(1, total, one, 0)
 
-    peers(lambda device: pl.semaphore_signal(barrier, inc=1, device_id=device, device_id_type=MESH))
+    def within(at, step, size):
+        return jnp.logical_and(at + step >= 0, at + step < size)
+
+    def spread(semaphore, reach, both_layers):
+        for a in (-reach, 0, reach):
+            for b in (-reach, 0, reach):
+                for c in range(nlayer if both_layers else 1):
+                    if (a, b, c) == (0, 0, 0) or abs(a) >= ngx or abs(b) >= ngy:
+                        continue
+
+                    @pl.when(jnp.logical_and(within(gx, a, ngx), within(gy, b, ngy)))
+                    def _():
+                        device = (lax.clamp(0, gx + a, ngx - 1), lax.clamp(0, gy + b, ngy - 1), other(layer, c, nlayer))
+                        pl.semaphore_signal(semaphore, inc=1, device_id=device, device_id_type=MESH)
+
+    def gathered(semaphore, reach, both_layers):
+        def count(at, size):
+            return 1 + (at >= reach).astype(jnp.int32) + (at + reach < size).astype(jnp.int32)
+
+        spots = count(gx, ngx) * count(gy, ngy)
+        pl.semaphore_wait(semaphore, spots * (nlayer if both_layers else 1) - 1)
+
+    spread(barrier, 1, True)
+    reaches = [1]
+    while 2 * reaches[-1] < max(ngx, ngy) - 1:
+        reaches.append(2 * reaches[-1])
 
     above, below, before, after = gx > 0, gx < ngx - 1, gy > 0, gy < ngy - 1
     gx_up, gx_down = lax.max(gx - 1, 0), lax.min(gx + 1, ngx - 1)
@@ -219,35 +249,36 @@
     plane_sends = []
     for k, ref in enumerate((metal_in, start_in)):
         at = pl.ds(k * nz + mine, nl)
-        for src, dst in (
-            (ref.at[:, pl.ds(other_row, half)], raw.at[at, pl.ds(0, half)]),
-            (ref.at[:, pl.ds(other_inner, SUB)], inner.at[at]),
-        ):
+        for src, dst in [
+            (ref.at[:, pl.ds(other_row, half), lanes_of[t]], raw.at[at, t, pl.ds(0, half)]) for t in range(flat)
+        ] + [(ref.at[:, pl.ds(other_inner, SUB)], inner.at[at])]:
             n = len(plane_sends)
             plane_sends.append(to_partner(src, dst, part_send.at[n], part_recv.at[n]))
 
-    for op in edge_loads:
-        op.wait()
     sub = lax.broadcasted_iota(jnp.int32, (SUB, nc), 0)
-    pairs = [(l, nl + l) for l in range(nl)] + [(2 * nl, 2 * nl + 1)]
-    for k, (a, b) in enumerate(pairs):
-        low = pltpu.roll(row_src[0, b], SUB // 2, 0)
-        row_pack[0, k] = jnp.where(sub < SUB // 2, row_src[0, a], low)
-        low = pltpu.roll(row_src[1, b], SUB // 2, 0)
-        row_pack[1, k] = jnp.where(sub < SUB // 2, low, row_src[1, a])
     lane = lax.broadcasted_iota(jnp.int32, (nr, LANES), 1)
     kinds = 2 * nl + 2
-    owner = ((lane + 4) >> 3) & (LANES // 8 - 1)
-    packed = jnp.ones((nr, LANES), jnp.float32)
-    for q in range(kinds):
-        pair = jnp.where(lane < LANES // 2, col_src[0, q], col_src[1, q])
-        if q:
-            pair = pltpu.roll(pair, 8 * q, 1)
-        packed = jnp.where(owner == q, pair, packed)
-    col_pack[...] = packed
+
+    def pack_edges():
+        for op in edge_loads:
+            op.wait()
+        pairs = [(l, nl + l) for l in range(nl)] + [(2 * nl, 2 * nl + 1)]
+        for k, (a, b) in enumerate(pairs):
+            low = pltpu.roll(row_src[0, b], SUB // 2, 0)
+            row_pack[0, k] = jnp.where(sub < SUB // 2, row_src[0, a], low)
+            low = pltpu.roll(row_src[1, b], SUB // 2, 0)
+            row_pack[1, k] = jnp.where(sub < SUB // 2, low, row_src[1, a])
+        owner = ((lane + 4) >> 3) & (LANES // 8 - 1)
+        packed = jnp.ones((nr, LANES), jnp.float32)
+        for q in range(kinds):
+            pair = jnp.where(lane < LANES // 2, col_src[0, q], col_src[1, q])
+            if q:
+                pair = pltpu.roll(pair, 8 * q, 1)
+            packed = jnp.where(owner == q, pair, packed)
+        col_pack[...] = packed
 
     tall_size = nr * halves
-    acc[...] = jnp.zeros_like(acc)
+    totals = [None] * PARTS
     ids = lax.broadcasted_iota(jnp.int32, (max(tall_size, WIDE), LANES), 0).astype(jnp.float32).astype(jnp.bfloat16)
     for op in slot_loads:
         op.wait()
@@ -257,30 +288,39 @@
     )
     nt = (((1,), (1,)), ((), ()))
     for i in range(chunks):
-        if i == min(BARRIER_AT, chunks - 1):
-            pl.semaphore_wait(barrier, total - 1)
+        if i == min(SEND_AT, chunks - 1):
+            pack_edges()
+            gathered(barrier, 1, True)
             begin(halo_sends)
             for op in plane_sends:
                 op.start()
+            spread(ready.at[0], 1, False)
         chunk_loads[i].wait()
-        amounts = lax.dot_general(wide_weight, pbuf[i], nt, preferred_element_type=jnp.float32)[0:1]
         position = i * slots + lax.broadcasted_iota(jnp.int32, (1, slots), 1)
-        amounts = jnp.where(position < live, amounts, 0.0).astype(jnp.bfloat16)
         cell = cells[i]
         column = rem_by(cell, nc)
         tall = div_by(column, WIDE) * nr + div_by(cell, nc)
         tall = tall.astype(jnp.float32).astype(jnp.bfloat16)
         short = rem_by(column, WIDE).astype(jnp.float32).astype(jnp.bfloat16)
-        left, right = [], []
         zero, one = jnp.zeros((), jnp.bfloat16), jnp.ones((), jnp.bfloat16)
-        for g in range(slots // LANES):
-            part = slice(g * LANES, (g + 1) * LANES)
-            left.append(jnp.where(ids[:tall_size] == tall[:, part], jnp.broadcast_to(amounts[:, part], (tall_size, LANES)), zero))
-            right.append(jnp.where(ids[:WIDE] == short[:, part], one, zero))
-        acc[...] += lax.dot_general(
-            jnp.concatenate(left, axis=1), jnp.concatenate(right, axis=1), nt,
-            preferred_element_type=jnp.float32,
-        ).reshape(acc.shape)
+        for k in range(PARTS):
+            block = slice(k * (slots // PARTS), (k + 1) * (slots // PARTS))
+            amounts = lax.dot_general(wide_weight, pbuf[i, block], nt, preferred_element_type=jnp.float32)[0:1]
+            amounts = jnp.where(position[:, block] < live, amounts, 0.0).astype(jnp.bfloat16)
+            left, right = [], []
+            for g in range(slots // PARTS // LANES):
+                part = slice(g * LANES, (g + 1) * LANES)
+                spot = slice(block.start + part.start, block.start + part.stop)
+                left.append(jnp.where(ids[:tall_size] == tall[:, spot], jnp.broadcast_to(amounts[:, part], (tall_size, LANES)), zero))
+                right.append(jnp.where(ids[:WIDE] == short[:, spot], one, zero))
+            product = lax.dot_general(
+                jnp.concatenate(left, axis=1), jnp.concatenate(right, axis=1).astype(jnp.float8_e4m3fn), nt,
+                preferred_element_type=jnp.float32,
+            )
+            totals[k] = product if totals[k] is None else totals[k] + product
+    for k in range(PARTS):
+        acc_parts[(layer + k) % PARTS] = totals[k].reshape(acc.shape)
+    acc[...] = functools.reduce(jnp.add, [acc_parts[k] for k in range(PARTS)])
 
     strips[0] = jnp.transpose(acc[0, :, pl.ds(0, LANES)])[0:SUB]
     strips[1] = jnp.transpose(acc[halves - 1, :, pl.ds(WIDE - LANES, LANES)])[LANES - SUB :]
@@ -299,20 +339,33 @@
     begin(cur_sends)
     cur_op.start()
 
+    gathered(ready.at[0], 1, False)
+    if len(reaches) > 1:
+        spread(ready.at[1], reaches[1], False)
+
     for op in own_loads:
         op.wait()
+    for l in range(nl):
+        for t in range(flat):
+            away_start[l, t, pl.ds(half, SUB)] = jnp.zeros((SUB, LANES), jnp.float32)
     for op in plane_sends:
         op.wait()
     receive(0, halo_arrivals, TINY)
     inward = (sub < SUB // 2) == first
+
+    def close(q, value):
+        value = jnp.where(inward, inner[q], value)
+        for t, at in enumerate(lanes_of):
+            raw[q, t, pl.ds(half, SUB)] = value[:, t * LANES : (t + 1) * LANES]
+
     for k in range(nlayer):
         for l in range(nl):
             got = row_recv[k, l]
             for q, value in ((k * nl + l, got), (nz + k * nl + l, pltpu.roll(got, SUB // 2, 0))):
-                raw[q, pl.ds(half, SUB)] = jnp.where(inward, inner[q], value)
+                close(q, value)
     got = row_recv[0, nl]
     for q, value in ((2 * nz, got), (2 * nz + 1, pltpu.roll(got, SUB // 2, 0))):
-        raw[q, pl.ds(half, SUB)] = jnp.where(inward, inner[q], value)
+        close(q, value)
     lane_half = lane[:half]
     lane_sub = lane[:SUB]
     inward_tile = inward[:, :LANES]
@@ -321,9 +374,6 @@
     body_at = pl.ds(pl.multiple_of(SUB * layer, SUB), half)
     inner_at = pl.ds(pl.multiple_of(half * (1 - layer), SUB), SUB)
     for k in range(nlayer):
-        def side_of(tall, cut, corner):
-            return jnp.where((cut & 7) < 4, tall[0], tall[1])
-
         main = jnp.where((lane_half & 7) < 4, col_recv[RIGHT, k, body_at], col_recv[LEFT, k, body_at])
         near = jnp.where((lane_sub & 7) < 4, col_recv[RIGHT, k, inner_at], col_recv[LEFT, k, inner_at])
         far = jnp.where((lane_sub & 7) < 4, corner_recv[RIGHT, k], corner_recv[LEFT, k])
@@ -333,18 +383,18 @@
             spots += [(2 * nl, 2 * nz), (2 * nl + 1, 2 * nz + 1)]
         for q, plane in spots:
             turned = pltpu.roll(mixed, LANES - 8 * q, 1) if q else mixed
-            edge[plane] = jnp.where(rim, turned, 1.0)
+            raw[plane, flat] = jnp.where(rim, turned, 1.0)
 
     shape = (tiles, high, SUB, LANES)
-    sub_at = lax.broadcasted_iota(jnp.int32, shape, 2)
     lane_at = lax.broadcasted_iota(jnp.int32, shape, 3)
-    last_sub, first_sub = sub_at == SUB - 1, sub_at == 0
     last_lane, first_lane = lane_at == LANES - 1, lane_at == 0
+    spill = lax.broadcasted_iota(jnp.int32, (SUB, LANES), 0) == SUB - 1
+
+    def comb(ref):
+        return jnp.stack([ref[pl.ds(v, SUB, stride=high), :] for v in range(high)])
 
     def plane_of(q):
-        value = raw[q]
-        parts = [value[:, t * LANES : (t + 1) * LANES] for t in range(flat)] + [edge[q]]
-        return jnp.stack([part.reshape(high, SUB, LANES) for part in parts])
+        return jnp.stack([comb(raw.at[q, t]) for t in range(tiles)])
 
     def keep(ref, at, value):
         ref[at] = value.reshape(tiles, ext, LANES)
@@ -353,12 +403,10 @@
         return ref[at].reshape(shape)
 
     def row_up(x):
-        y = pltpu.roll(x.reshape(tiles * high, SUB, LANES), SUB - 1, 1).reshape(shape)
-        return jnp.where(last_sub, jnp.concatenate([y[:, 1:], y[:, :1]], axis=1), y)
+        return jnp.concatenate([x[:, 1:], pltpu.roll(x[:, 0], SUB - 1, 1)[:, None]], axis=1)
 
     def row_down(x):
-        y = pltpu.roll(x.reshape(tiles * high, SUB, LANES), 1, 1).reshape(shape)
-        return jnp.where(first_sub, jnp.concatenate([y[:, -1:], y[:, :-1]], axis=1), y)
+        return jnp.concatenate([pltpu.roll(x[:, -1], 1, 1)[:, None], x[:, :-1]], axis=1)
 
     def lane_up(x):
         y = pltpu.roll(x.reshape(tiles * ext, LANES), LANES - 1, 1).reshape(shape)
@@ -380,10 +428,13 @@
     moments = [None] * (2 * ITERS)
 
     def measure(j, left, right):
-        own = (left * right)[:flat, : half // SUB]
-        value = jnp.sum(own.reshape(flat * (half // SUB), SUB, LANES), axis=0)
+        both = (left * right)[:flat]
+        most = jnp.sum(both[:, 1:].reshape(flat * (high - 1), SUB, LANES), axis=0)
+        value = jnp.sum(both[:, 0], axis=0) + jnp.where(spill, 0.0, most)
         moments[j] = value if moments[j] is None else moments[j] + value
 
+    for z in range(nz):
+        keep(began, z, plane_of(nz + z))
     via = plane_of(2 * nz)
     resist = 0.5 / plane_of(0)
     for z in range(nz):
@@ -404,8 +455,8 @@
             whole = whole + plane_of(2 * nz + 1)
         inverse = 1.0 / whole
         keep(dinv, z, inverse)
-        value = plane_of(nz + z)
-        image = pull(z, value, plane_of(nz + z + 1) if z + 1 < nz else None, plane_of(nz + z - 1) if z else None)
+        value = held(began, z)
+        image = pull(z, value, held(began, z + 1) if z + 1 < nz else None, held(began, z - 1) if z else None)
         image = image - whole * value
         keep(grad.at[0], z, image)
         if z:
@@ -414,7 +465,7 @@
             measure(0, scaled, image)
 
     back = [
-        to_partner(src.at[pl.ds(theirs, nl), pl.ds(0, flat), pl.ds(0, half)], dst, back_send.at[k], back_recv.at[k])
+        to_partner(src.at[pl.ds(theirs, nl), pl.ds(0, flat)], dst, back_send.at[k], back_recv.at[k])
         for k, (src, dst) in enumerate([(grad.at[c], away.at[c]) for c in range(ITERS + 1)] + [(dinv, away_dinv)])
     ]
     back[ITERS + 1].start()
@@ -461,7 +512,7 @@
             )
         cur[t, pl.ds(0, half)] = main
         cur[t, pl.ds(half, SUB)] = jnp.where(inward_tile, near, far)
-    image = held(grad.at[0], 0) + cur[...].reshape(shape)
+    image = held(grad.at[0], 0) + jnp.stack([comb(cur.at[t]) for t in range(tiles)])
     keep(grad.at[0], 0, image)
     scaled = held(dinv, 0) * image
     keep(field.at[0], 0, scaled)
@@ -479,6 +530,10 @@
         packed = jnp.where(row == j, jnp.sum(one_row, axis=1, keepdims=True), packed)
     sums[...] = packed
     gather[me] = packed
+    for k in range(1, len(reaches)):
+        gathered(ready.at[k], reaches[k], False)
+        if k + 1 < len(reaches):
+            spread(ready.at[k + 1], reaches[k + 1], False)
     peers(
         lambda device: pltpu.make_async_remote_copy(
             src_ref=sums, dst_ref=gather.at[me], send_sem=gsend, recv_sem=grecv,
@@ -495,24 +550,36 @@
     summed = jnp.sum(gather[...], axis=0)
     totals = [jnp.sum(jnp.where(row == j, summed, 0.0), axis=1, keepdims=True) for j in range(2 * ITERS)]
     moved, scaled = cg_coefficients(totals)
-    own_out = pl.ds(pl.multiple_of(own_row, SUB), half)
-    other_out = pl.ds(pl.multiple_of(other_row, SUB), half)
     for l in range(nl):
         for t in range(flat):
-            at = pl.ds(t * LANES, LANES)
-            own = pl.ds(0, half)
-            for place, parts, inverse, start in (
-                (own_out, [grad[c, mine + l, t, own] for c in range(ITERS + 1)], dinv[mine + l, t, own], raw[nz + mine + l, own, at]),
-                (other_out, [away[c, l, t] for c in range(ITERS + 1)], away_dinv[l, t], away_start[l, :, at]),
+            for h, parts, inverse, start in (
+                (layer, [grad[c, mine + l, t] for c in range(ITERS + 1)], dinv[mine + l, t], began[mine + l, t]),
+                (1 - layer, [away[c, l, t] for c in range(ITERS + 1)], away_dinv[l, t], comb(away_start.at[l, t])),
             ):
+                parts = [part.reshape(high, SUB, LANES) for part in parts]
                 step = moved[0] * parts[0]
                 for c in range(1, ITERS):
                     step = step + moved[c] * parts[c]
-                drop[l, place, at] = start + inverse * step
+                step = start.reshape(high, SUB, LANES) + inverse.reshape(high, SUB, LANES) * step
                 rest = scaled[0] * parts[0]
                 for c in range(1, ITERS + 1):
                     rest = rest + scaled[c] * parts[c]
-                residual[l, place, at] = rest
+                for v in range(high):
+                    drop[h, l, t, pl.ds(v, SUB, stride=high), :] = step[v]
+                    residual[h, l, t, pl.ds(v, SUB, stride=high), :] = rest[v]
+
+
+def put(half, drop_in, residual_in, drop, residual, sem):
+    ops = []
+    for src, dst in ((drop_in, drop), (residual_in, residual)):
+        for h in range(src.shape[0]):
+            for t in range(src.shape[2]):
+                place = dst.at[:, pl.ds(h * half, half), pl.ds(t * LANES, LANES)]
+                ops.append(pltpu.make_async_copy(src.at[h, :, t, pl.ds(0, half)], place, sem.at[len(ops)]))
+    for op in ops:
+        op.start()
+    for op in ops:
+        op.wait()
 
 
 def per_device(sizes, profiles, time_weight, slot_cell, inst_count, metal, via_density, pad, start_drop):
@@ -534,9 +601,10 @@
         return pltpu.VMEM(shape, jnp.float32)
 
     DMA = pltpu.SemaphoreType.DMA
-    return pl.pallas_call(
+    tiled = jax.ShapeDtypeStruct((nlayer, nl, tiles - 1, ext, LANES), jnp.float32)
+    results = pl.pallas_call(
         functools.partial(kernel, sizes, slots),
-        out_shape=(out, out),
+        out_shape=(tiled, tiled),
         in_specs=[hbm, hbm, hbm, vmem, hbm, hbm, hbm, hbm],
         out_specs=(vmem, vmem),
         scratch_shapes=[
@@ -544,9 +612,8 @@
             pltpu.VMEM((chunks, 1, slots), jnp.int32),
             pltpu.VMEM((chunks, slots, times), jnp.bfloat16),
             DMA((chunks,)),
-            DMA((27,)),
-            room(2 * nz + 2, ext, nc),
-            room(2 * nz + 2, ext, LANES),
+            DMA((22 + 5 * (tiles - 1),)),
+            room(2 * nz + 2, tiles, ext, LANES),
             room(2 * nz + 2, SUB, nc),
             room(2, kinds, SUB, nc),
             room(2, kinds, nr, LANES),
@@ -555,6 +622,7 @@
             room(nlayer, pairs, SUB, nc),
             room(2, nlayer, ext, LANES),
             room(2, nlayer, SUB, LANES),
+            room(PARTS, halves, nr, WIDE),
             room(halves, nr, WIDE),
             room(2, SUB, nr),
             room(halves, ext, WIDE),
@@ -565,23 +633,25 @@
             room(tiles, ext, LANES),
             room(nz, tiles, ext, LANES),
             room(nz, tiles, ext, LANES),
+            room(nz, tiles, ext, LANES),
             room(nz - 1, tiles, ext, LANES),
             room(nz, tiles, ext, LANES),
             room(ITERS, nz, tiles, ext, LANES),
             room(count, nz, tiles, ext, LANES),
-            room(count, nl, tiles - 1, half, LANES),
-            room(nl, tiles - 1, half, LANES),
-            room(nl, half, nc),
+            room(count, nl, tiles - 1, ext, LANES),
+            room(nl, tiles - 1, ext, LANES),
+            room(nl, tiles - 1, ext, LANES),
             room(1, LANES),
             room(total, 1, LANES),
             DMA((2, 10)),
             DMA((2, 10)),
-            DMA((5,)),
-            DMA((5,)),
+            DMA((2 * tiles + 1,)),
+            DMA((2 * tiles + 1,)),
             DMA((count + 1,)),
             DMA((count + 1,)),
             DMA,
             DMA,
+            pltpu.SemaphoreType.REGULAR((max(sizes[:2]).bit_length(),)),
         ],
         compiler_params=pltpu.CompilerParams(
             collective_id=0, has_side_effects=True, vmem_limit_bytes=48 * 1024 * 1024
@@ -591,6 +661,13 @@
         stay(slot_cell.reshape(chunks, 1, slots)), inst_count,
         stay(metal), stay(via_density), stay(pad), stay(start_drop),
     )
+    return pl.pallas_call(
+        functools.partial(put, half),
+        out_shape=(out, out),
+        in_specs=[vmem, vmem],
+        out_specs=(hbm, hbm),
+        scratch_shapes=[DMA((4 * (tiles - 1),))],
+    )(*[pltpu.with_memory_space_constraint(result, memory_space=pltpu.VMEM) for result in results])
 
 
 def solution(mesh):

time: 28.6 us -> 28.1 us (0.983)
  local copies, waits for them, and re-layouts: 1.76 us -> 0 us
  Pallas kernels: 25.4 us -> 26.7 us
    unnamed x2 -> x0, local copies, waits for them, and re-layouts: 1.76 us -> none
    pallas_call x1 -> x2, Pallas kernels: 25.4 us -> 26.7 us  [the longest x1 25.4 us: per_device(): pl.pallas_call(functools.partial(kernel, sizes, slots), out_shape=(tiled,...]
where the time goes in v2:
time: 28.1 us; the launch traced here: 27.9 us
  Pallas kernels  26.7 us (95%)
  between operations  1.29 us (5%)
    pallas_call x1, Pallas kernels, per_device(): pl.pallas_call(functools.partial(kernel, sizes, slots), out_shape=(tiled,...  25.4 us
    pallas_call x1, Pallas kernels, per_device(): pl.pallas_call(functools.partial(put, half), out_shape=(out, out), in_spe...  1.27 us

profile of v2, /device:TPU:0, one launch (start us, length us, event | category | flops | bytes accessed | tf_op | source)
XLA Modules:
  0.0 27.9 jit_solution(3264517929821381662)
XLA Ops:
  1.3 25.4 %shard_map.95 = (f32[2,3,4,72,128]{4,3,2,1,0:T(8,128)S(1)}, f32[2,3,4,72,128]{4,3,2,1,0:T(8,128)S(1)}) custom-call(bf16[16,1024,256]{2,1,0:T(8,128)(2,1)} %bitcast.3, bf16[2,128]{1,0:T(2,128)(2,1)} %bitcast.5, s32[16,1,1024]{2,1,0:T(1,128)} %bitcast.4, s32[1,1,1]{2,1,0:T(1,128)S(6)} %copy.10.count, f32[3,128,512]{2,1,0:T(8,128)} %metal_in.1, ...), custom_call_target="tpu_custom_call" | custom-call | tf_op jit(solution)/shard_map/pallas_call | solution.py:605
  26.7 1.3 %shard_map.96 = (f32[3,128,512]{2,1,0:T(8,128)}, f32[3,128,512]{2,1,0:T(8,128)}) custom-call(f32[2,3,4,72,128]{4,3,2,1,0:T(8,128)S(1)} %get-tuple-element.4.drop_in, f32[2,3,4,72,128]{4,3,2,1,0:T(8,128)S(1)} %get-tuple-element.5.residual_in), custom_call_target="tpu_custom_call" | custom-call | tf_op jit(solution)/shard_map/pallas_call | solution.py:664

commit v3 on v2

--- a/solution.py
+++ b/solution.py
@@ -14,6 +14,7 @@
 TINY = 5e-31
 SEND_AT = 1
 PARTS = 2
+GROUP = 4
 MESH = pl.DeviceIdType.MESH
 
 
@@ -67,7 +68,7 @@
     weight, cells, pbuf, psem, isem,
     raw, inner, row_src, col_src, row_pack, col_pack, row_recv, col_recv, corner_recv,
     acc_parts, acc, strips, cur_recv, cur_row, cur_col, cur_corner, col_turn, cur,
-    began, rows_link, cols_link, up_link, dinv, field, grad, away, away_dinv, away_start,
+    began, resist, flat_planes, rows_link, cols_link, up_link, dinv, field, grad, moments, away, away_dinv, away_start,
     sums, gather, send_sem, recv_sem, part_send, part_recv, back_send, back_recv, gsend, grecv, ready,
 ):
     ngx, ngy, nlayer = sizes
@@ -128,7 +129,7 @@
     for t, at in enumerate(lanes_of):
         own_loads.append(load(start_in.at[:, pl.ds(other_row, half), at], away_start.at[:, t, pl.ds(0, half)]))
     chunk_loads = [pltpu.make_async_copy(profiles.at[i], pbuf.at[i], psem.at[i]) for i in range(chunks)]
-    for op in slot_loads + chunk_loads[:2] + edge_loads + chunk_loads[2:] + own_loads:
+    for op in slot_loads + chunk_loads[:GROUP] + edge_loads + chunk_loads[GROUP:] + own_loads:
         op.start()
 
     barrier = pltpu.get_barrier_semaphore()
@@ -278,7 +279,6 @@
         col_pack[...] = packed
 
     tall_size = nr * halves
-    totals = [None] * PARTS
     ids = lax.broadcasted_iota(jnp.int32, (max(tall_size, WIDE), LANES), 0).astype(jnp.float32).astype(jnp.bfloat16)
     for op in slot_loads:
         op.wait()
@@ -287,39 +287,54 @@
         [jnp.broadcast_to(weight[k : k + 1], (16, weight.shape[1])) for k in range(weight.shape[0])], axis=1
     )
     nt = (((1,), (1,)), ((), ()))
-    for i in range(chunks):
-        if i == min(SEND_AT, chunks - 1):
+    group = min(GROUP, chunks)
+    acc_parts[...] = jnp.zeros_like(acc_parts)
+
+    def scatter(step, carry):
+        @pl.when(step == min(SEND_AT, chunks // group - 1))
+        def _():
             pack_edges()
             gathered(barrier, 1, True)
             begin(halo_sends)
             for op in plane_sends:
                 op.start()
             spread(ready.at[0], 1, False)
-        chunk_loads[i].wait()
-        position = i * slots + lax.broadcasted_iota(jnp.int32, (1, slots), 1)
-        cell = cells[i]
-        column = rem_by(cell, nc)
-        tall = div_by(column, WIDE) * nr + div_by(cell, nc)
-        tall = tall.astype(jnp.float32).astype(jnp.bfloat16)
-        short = rem_by(column, WIDE).astype(jnp.float32).astype(jnp.bfloat16)
+
+        totals = [None] * PARTS
         zero, one = jnp.zeros((), jnp.bfloat16), jnp.ones((), jnp.bfloat16)
+        for u in range(group):
+            i = step * group + u
+            pltpu.make_async_copy(profiles.at[i], pbuf.at[i], psem.at[i]).wait()
+        for u in range(group):
+            i = step * group + u
+            position = i * slots + lax.broadcasted_iota(jnp.int32, (1, slots), 1)
+            cell = cells[i]
+            column = rem_by(cell, nc)
+            tall = div_by(column, WIDE) * nr + div_by(cell, nc)
+            tall = tall.astype(jnp.float32).astype(jnp.bfloat16)
+            short = rem_by(column, WIDE).astype(jnp.float32).astype(jnp.bfloat16)
+            for k in range(PARTS):
+                size = slots // PARTS
+                amounts = lax.dot_general(
+                    wide_weight, pbuf[i, k * size : (k + 1) * size], nt, preferred_element_type=jnp.float32
+                )[0:1]
+                amounts = jnp.where(position[:, k * size : (k + 1) * size] < live, amounts, 0.0).astype(jnp.bfloat16)
+                left, right = [], []
+                for g in range(size // LANES):
+                    part = slice(g * LANES, (g + 1) * LANES)
+                    spot = slice(k * size + part.start, k * size + part.stop)
+                    left.append(jnp.where(ids[:tall_size] == tall[:, spot], jnp.broadcast_to(amounts[:, part], (tall_size, LANES)), zero))
+                    right.append(jnp.where(ids[:WIDE] == short[:, spot], one, zero))
+                product = lax.dot_general(
+                    jnp.concatenate(left, axis=1), jnp.concatenate(right, axis=1).astype(jnp.float8_e4m3fn), nt,
+                    preferred_element_type=jnp.float32,
+                )
+                totals[k] = product if totals[k] is None else totals[k] + product
         for k in range(PARTS):
-            block = slice(k * (slots // PARTS), (k + 1) * (slots // PARTS))
-            amounts = lax.dot_general(wide_weight, pbuf[i, block], nt, preferred_element_type=jnp.float32)[0:1]
-            amounts = jnp.where(position[:, block] < live, amounts, 0.0).astype(jnp.bfloat16)
-            left, right = [], []
-            for g in range(slots // PARTS // LANES):
-                part = slice(g * LANES, (g + 1) * LANES)
-                spot = slice(block.start + part.start, block.start + part.stop)
-                left.append(jnp.where(ids[:tall_size] == tall[:, spot], jnp.broadcast_to(amounts[:, part], (tall_size, LANES)), zero))
-                right.append(jnp.where(ids[:WIDE] == short[:, spot], one, zero))
-            product = lax.dot_general(
-                jnp.concatenate(left, axis=1), jnp.concatenate(right, axis=1).astype(jnp.float8_e4m3fn), nt,
-                preferred_element_type=jnp.float32,
-            )
-            totals[k] = product if totals[k] is None else totals[k] + product
-    for k in range(PARTS):
-        acc_parts[(layer + k) % PARTS] = totals[k].reshape(acc.shape)
+            acc_parts[k] += totals[k].reshape(acc.shape)
+        return carry
+
+    lax.fori_loop(0, chunks // group, scatter, 0)
     acc[...] = functools.reduce(jnp.add, [acc_parts[k] for k in range(PARTS)])
 
     strips[0] = jnp.transpose(acc[0, :, pl.ds(0, LANES)])[0:SUB]
@@ -416,74 +431,94 @@
         y = pltpu.roll(x.reshape(tiles * ext, LANES), 1, 1).reshape(shape)
         return jnp.where(first_lane, jnp.concatenate([y[-1:], y[:-1]], axis=0), y)
 
-    def pull(z, value, upper, lower):
+    def pull(z, source):
         rows, cols = held(rows_link, z), held(cols_link, z)
+        value = held(source, z + 1)
         out = rows * row_up(value) + row_down(rows * value) + cols * lane_up(value) + lane_down(cols * value)
-        if upper is not None:
-            out = out + held(up_link, z) * upper
-        if lower is not None:
-            out = out + held(up_link, z - 1) * lower
-        return out
-
-    moments = [None] * (2 * ITERS)
+        return value, out + held(up_link, z + 1) * held(source, z + 2) + held(up_link, z) * held(source, z)
 
     def measure(j, left, right):
         both = (left * right)[:flat]
         most = jnp.sum(both[:, 1:].reshape(flat * (high - 1), SUB, LANES), axis=0)
-        value = jnp.sum(both[:, 0], axis=0) + jnp.where(spill, 0.0, most)
-        moments[j] = value if moments[j] is None else moments[j] + value
-
+        moments[j] += jnp.sum(both[:, 0], axis=0) + jnp.where(spill, 0.0, most)
+
+    blank = jnp.zeros((tiles, ext, LANES), jnp.float32)
+    moments[...] = jnp.zeros_like(moments)
+    for at in (0, nz + 1):
+        began[at] = blank
+    for c in range(ITERS):
+        for at in (0, nz + 1):
+            field[c, at] = blank
+    resist[0] = jnp.full((tiles, ext, LANES), 0.5 / TINY, jnp.float32)
+    up_link[nz] = blank
+    for k in range(2):
+        keep(flat_planes, k, plane_of(2 * nz + k))
     for z in range(nz):
-        keep(began, z, plane_of(nz + z))
-    via = plane_of(2 * nz)
-    resist = 0.5 / plane_of(0)
-    for z in range(nz):
-        keep(rows_link, z, 1.0 / (resist + row_up(resist)))
-        keep(cols_link, z, 1.0 / (resist + lane_up(resist)))
-        if z + 1 < nz:
-            upper = 0.5 / plane_of(z + 1)
-            keep(up_link, z, via / (resist + upper))
-            resist = upper
-    for z in range(nz):
+        keep(resist, z + 1, plane_of(z))
+        keep(began, z + 1, plane_of(nz + z))
+    for l in range(nl):
+        for t in range(flat):
+            away_start[l, t] = comb(away_start.at[l, t]).reshape(ext, LANES)
+
+    def links(z, carry):
+        value = 0.5 / held(resist, z + 1)
+        keep(resist, z + 1, value)
+        keep(rows_link, z, 1.0 / (value + row_up(value)))
+        keep(cols_link, z, 1.0 / (value + lane_up(value)))
+        keep(up_link, z, held(flat_planes, 0) / (held(resist, z) + value))
+        return carry
+
+    lax.fori_loop(0, nz, links, 0)
+
+    def opening(z, carry):
         rows, cols = held(rows_link, z), held(cols_link, z)
-        whole = rows + row_down(rows) + cols + lane_down(cols)
-        if z + 1 < nz:
-            whole = whole + held(up_link, z)
-        if z:
-            whole = whole + held(up_link, z - 1)
-        if z + 1 == nz:
-            whole = whole + plane_of(2 * nz + 1)
+        whole = rows + row_down(rows) + cols + lane_down(cols) + held(up_link, z) + held(up_link, z + 1)
+        whole = whole + jnp.where(z == nz - 1, held(flat_planes, 1), 0.0)
         inverse = 1.0 / whole
         keep(dinv, z, inverse)
-        value = held(began, z)
-        image = pull(z, value, held(began, z + 1) if z + 1 < nz else None, held(began, z - 1) if z else None)
+        value, image = pull(z, began)
         image = image - whole * value
         keep(grad.at[0], z, image)
-        if z:
-            scaled = inverse * image
-            keep(field.at[0], z, scaled)
+        scaled = inverse * image
+        keep(field.at[0], z + 1, scaled)
+
+        @pl.when(z > 0)
+        def _():
             measure(0, scaled, image)
 
-    back = [
-        to_partner(src.at[pl.ds(theirs, nl), pl.ds(0, flat)], dst, back_send.at[k], back_recv.at[k])
-        for k, (src, dst) in enumerate([(grad.at[c], away.at[c]) for c in range(ITERS + 1)] + [(dinv, away_dinv)])
-    ]
-    back[ITERS + 1].start()
+        return carry
+
+    lax.fori_loop(0, nz, opening, 0)
+
+    def back(c):
+        src, dst = (dinv, away_dinv) if c is None else (grad.at[c], away.at[c])
+        k = ITERS + 1 if c is None else c
+        return to_partner(src.at[pl.ds(theirs, nl), pl.ds(0, flat)], dst, back_send.at[k], back_recv.at[k])
+
+    back(None).start()
 
     def advance(c, z):
-        source = field.at[c - 1]
-        value = held(source, z)
-        image = pull(z, value, held(source, z + 1) if z + 1 < nz else None, held(source, z - 1) if z else None)
+        value, image = pull(z, field.at[c - 1])
         keep(grad.at[c], z, image)
+        scaled = held(dinv, z) * image
+        keep(field.at[c], z + 1, scaled)
         measure(2 * c - 1, value, image)
-        if c < ITERS:
-            scaled = held(dinv, z) * image
-            keep(field.at[c], z, scaled)
-            measure(2 * c, scaled, image)
-
-    for c in range(1, ITERS + 1):
-        for z in range(c + 1, nz):
-            advance(c, z)
+        measure(2 * c, scaled, image)
+
+    def sweep(lowest, highest, finish):
+        def outer(c, carry):
+            def step(z, inner_carry):
+                advance(c, z)
+                return inner_carry
+
+            lax.fori_loop(lowest(c), highest(c), step, 0)
+            if finish:
+                back(c).start()
+            return carry
+
+        lax.fori_loop(1, ITERS + 1, outer, 0)
+
+    sweep(lambda c: c + 1, lambda c: nz, False)
 
     cur_op.wait()
     receive(1, cur_arrivals, 0.0)
@@ -515,17 +550,15 @@
     image = held(grad.at[0], 0) + jnp.stack([comb(cur.at[t]) for t in range(tiles)])
     keep(grad.at[0], 0, image)
     scaled = held(dinv, 0) * image
-    keep(field.at[0], 0, scaled)
+    keep(field.at[0], 1, scaled)
     measure(0, scaled, image)
-    back[0].start()
-    for c in range(1, ITERS + 1):
-        for z in range(min(c + 1, nz)):
-            advance(c, z)
-        back[c].start()
+    back(0).start()
+    sweep(lambda c: 0, lambda c: c + 1, True)
 
     row = lax.broadcasted_iota(jnp.int32, (1, LANES), 1)
     packed = jnp.zeros((1, LANES), jnp.float32)
-    for j, tile in enumerate(moments):
+    for j in range(2 * ITERS):
+        tile = moments[j]
         one_row = jnp.sum(tile, axis=0, keepdims=True)
         packed = jnp.where(row == j, jnp.sum(one_row, axis=1, keepdims=True), packed)
     sums[...] = packed
@@ -540,8 +573,8 @@
             device_id=device, device_id_type=MESH,
         ).start()
     )
-    for op in back:
-        op.wait()
+    for c in [*range(ITERS + 1), None]:
+        back(c).wait()
     sent(halo_sends)
     sent(cur_sends)
     most = gather.at[pl.ds(0, total - 1)]
@@ -550,23 +583,26 @@
     summed = jnp.sum(gather[...], axis=0)
     totals = [jnp.sum(jnp.where(row == j, summed, 0.0), axis=1, keepdims=True) for j in range(2 * ITERS)]
     moved, scaled = cg_coefficients(totals)
-    for l in range(nl):
-        for t in range(flat):
-            for h, parts, inverse, start in (
-                (layer, [grad[c, mine + l, t] for c in range(ITERS + 1)], dinv[mine + l, t], began[mine + l, t]),
-                (1 - layer, [away[c, l, t] for c in range(ITERS + 1)], away_dinv[l, t], comb(away_start.at[l, t])),
-            ):
-                parts = [part.reshape(high, SUB, LANES) for part in parts]
-                step = moved[0] * parts[0]
-                for c in range(1, ITERS):
-                    step = step + moved[c] * parts[c]
-                step = start.reshape(high, SUB, LANES) + inverse.reshape(high, SUB, LANES) * step
-                rest = scaled[0] * parts[0]
-                for c in range(1, ITERS + 1):
-                    rest = rest + scaled[c] * parts[c]
-                for v in range(high):
-                    drop[h, l, t, pl.ds(v, SUB, stride=high), :] = step[v]
-                    residual[h, l, t, pl.ds(v, SUB, stride=high), :] = rest[v]
+    def close_tile(k, carry):
+        l, t = k // flat, k % flat
+        for h, parts, inverse, start in (
+            (layer, [grad[c, mine + l, t] for c in range(ITERS + 1)], dinv[mine + l, t], began[mine + l + 1, t]),
+            (1 - layer, [away[c, l, t] for c in range(ITERS + 1)], away_dinv[l, t], away_start[l, t]),
+        ):
+            parts = [part.reshape(high, SUB, LANES) for part in parts]
+            step = moved[0] * parts[0]
+            for c in range(1, ITERS):
+                step = step + moved[c] * parts[c]
+            step = start.reshape(high, SUB, LANES) + inverse.reshape(high, SUB, LANES) * step
+            rest = scaled[0] * parts[0]
+            for c in range(1, ITERS + 1):
+                rest = rest + scaled[c] * parts[c]
+            for v in range(high):
+                drop[h, l, t, pl.ds(v, SUB, stride=high), :] = step[v]
+                residual[h, l, t, pl.ds(v, SUB, stride=high), :] = rest[v]
+        return carry
+
+    lax.fori_loop(0, nl * flat, close_tile, 0)
 
 
 def put(half, drop_in, residual_in, drop, residual, sem):
@@ -631,13 +667,16 @@
             room(2, nlayer, SUB, LANES),
             room(nr, LANES),
             room(tiles, ext, LANES),
+            room(nz + 2, tiles, ext, LANES),
+            room(nz + 1, tiles, ext, LANES),
+            room(2, tiles, ext, LANES),
             room(nz, tiles, ext, LANES),
             room(nz, tiles, ext, LANES),
+            room(nz + 1, tiles, ext, LANES),
             room(nz, tiles, ext, LANES),
-            room(nz - 1, tiles, ext, LANES),
-            room(nz, tiles, ext, LANES),
-            room(ITERS, nz, tiles, ext, LANES),
+            room(count, nz + 2, tiles, ext, LANES),
             room(count, nz, tiles, ext, LANES),
+            room(2 * count, SUB, LANES),
             room(count, nl, tiles - 1, ext, LANES),
             room(nl, tiles - 1, ext, LANES),
             room(nl, tiles - 1, ext, LANES),

time: 28.1 us -> 29.8 us (1.060)
  Pallas kernels: 26.7 us -> 28.4 us
    pallas_call x1, Pallas kernels: 25.4 us -> 27.1 us  [per_device(): pl.pallas_call(functools.partial(kernel, sizes, slots), out_shape=(tiled,...]
where the time goes in v3:
time: 29.8 us; the launch traced here: 29.6 us
  Pallas kernels  28.4 us (95%)
  between operations  1.29 us (4%)
    pallas_call x1, Pallas kernels, per_device(): pl.pallas_call(functools.partial(kernel, sizes, slots), out_shape=(tiled,...  27.1 us
    pallas_call x1, Pallas kernels, per_device(): pl.pallas_call(functools.partial(put, half), out_shape=(out, out), in_spe...  1.27 us

profile of v3, /device:TPU:0, one launch (start us, length us, event | category | flops | bytes accessed | tf_op | source)
XLA Modules:
  0.0 29.6 jit_solution(5926925496961562100)
XLA Ops:
  1.3 27.1 %shard_map.95 = (f32[2,3,4,72,128]{4,3,2,1,0:T(8,128)S(1)}, f32[2,3,4,72,128]{4,3,2,1,0:T(8,128)S(1)}) custom-call(bf16[16,1024,256]{2,1,0:T(8,128)(2,1)} %bitcast.3, bf16[2,128]{1,0:T(2,128)(2,1)} %bitcast.5, s32[16,1,1024]{2,1,0:T(1,128)} %bitcast.4, s32[1,1,1]{2,1,0:T(1,128)S(6)} %copy.10.count, f32[3,128,512]{2,1,0:T(8,128)} %metal_in.1, ...), custom_call_target="tpu_custom_call" | custom-call | tf_op jit(solution)/shard_map/pallas_call | solution.py:641
  28.4 1.3 %shard_map.96 = (f32[3,128,512]{2,1,0:T(8,128)}, f32[3,128,512]{2,1,0:T(8,128)}) custom-call(f32[2,3,4,72,128]{4,3,2,1,0:T(8,128)S(1)} %get-tuple-element.4.drop_in, f32[2,3,4,72,128]{4,3,2,1,0:T(8,128)S(1)} %get-tuple-element.5.residual_in), custom_call_target="tpu_custom_call" | custom-call | tf_op jit(solution)/shard_map/pallas_call | solution.py:703

commit v4 on v2

--- a/solution.py
+++ b/solution.py
@@ -12,7 +12,8 @@
 SUB = 8
 WIDE = 256
 TINY = 5e-31
-SEND_AT = 1
+SEND_AT = 3
+DEPTH = 4
 PARTS = 2
 MESH = pl.DeviceIdType.MESH
 
@@ -128,7 +129,7 @@
     for t, at in enumerate(lanes_of):
         own_loads.append(load(start_in.at[:, pl.ds(other_row, half), at], away_start.at[:, t, pl.ds(0, half)]))
     chunk_loads = [pltpu.make_async_copy(profiles.at[i], pbuf.at[i], psem.at[i]) for i in range(chunks)]
-    for op in slot_loads + chunk_loads[:2] + edge_loads + chunk_loads[2:] + own_loads:
+    for op in slot_loads + chunk_loads[:DEPTH]:
         op.start()
 
     barrier = pltpu.get_barrier_semaphore()
@@ -296,6 +297,8 @@
                 op.start()
             spread(ready.at[0], 1, False)
         chunk_loads[i].wait()
+        for op in chunk_loads[i + DEPTH : i + DEPTH + 1] + (edge_loads if i == 0 else []) + (own_loads if i == min(5, chunks - 1) else []):
+            op.start()
         position = i * slots + lax.broadcasted_iota(jnp.int32, (1, slots), 1)
         cell = cells[i]
         column = rem_by(cell, nc)

time: 28.1 us -> 26.7 us (0.950)
  Pallas kernels: 26.7 us -> 25.2 us
    pallas_call x1, Pallas kernels: 25.4 us -> 23.9 us  [per_device(): pl.pallas_call(functools.partial(kernel, sizes, slots), out_shape=(tiled,...]
where the time goes in v4:
time: 26.7 us; the launch traced here: 26.5 us
  Pallas kernels  25.2 us (94%)
  between operations  1.29 us (5%)
    pallas_call x1, Pallas kernels, per_device(): pl.pallas_call(functools.partial(kernel, sizes, slots), out_shape=(tiled,...  23.9 us
    pallas_call x1, Pallas kernels, per_device(): pl.pallas_call(functools.partial(put, half), out_shape=(out, out), in_spe...  1.27 us

profile of v4, /device:TPU:0, one launch (start us, length us, event | category | flops | bytes accessed | tf_op | source)
XLA Modules:
  0.0 26.5 jit_solution(1425978001194939993)
XLA Ops:
  1.3 23.9 %shard_map.95 = (f32[2,3,4,72,128]{4,3,2,1,0:T(8,128)S(1)}, f32[2,3,4,72,128]{4,3,2,1,0:T(8,128)S(1)}) custom-call(bf16[16,1024,256]{2,1,0:T(8,128)(2,1)} %bitcast.3, bf16[2,128]{1,0:T(2,128)(2,1)} %bitcast.5, s32[16,1,1024]{2,1,0:T(1,128)} %bitcast.4, s32[1,1,1]{2,1,0:T(1,128)S(6)} %copy.10.count, f32[3,128,512]{2,1,0:T(8,128)} %metal_in.1, ...), custom_call_target="tpu_custom_call" | custom-call | tf_op jit(solution)/shard_map/pallas_call | solution.py:608
  25.2 1.3 %shard_map.96 = (f32[3,128,512]{2,1,0:T(8,128)}, f32[3,128,512]{2,1,0:T(8,128)}) custom-call(f32[2,3,4,72,128]{4,3,2,1,0:T(8,128)S(1)} %get-tuple-element.4.drop_in, f32[2,3,4,72,128]{4,3,2,1,0:T(8,128)S(1)} %get-tuple-element.5.residual_in), custom_call_target="tpu_custom_call" | custom-call | tf_op jit(solution)/shard_map/pallas_call | solution.py:667

commit v5 on v4

--- a/solution.py
+++ b/solution.py
@@ -12,7 +12,7 @@
 SUB = 8
 WIDE = 256
 TINY = 5e-31
-SEND_AT = 3
+SEND_AT = 4
 DEPTH = 4
 PARTS = 2
 MESH = pl.DeviceIdType.MESH
@@ -288,6 +288,39 @@
         [jnp.broadcast_to(weight[k : k + 1], (16, weight.shape[1])) for k in range(weight.shape[0])], axis=1
     )
     nt = (((1,), (1,)), ((), ()))
+    size = slots // PARTS
+
+    def amounts_of(i):
+        position = i * slots + lax.broadcasted_iota(jnp.int32, (1, slots), 1)
+        out = []
+        for k in range(PARTS):
+            block = slice(k * size, (k + 1) * size)
+            amounts = lax.dot_general(wide_weight, pbuf[i, block], nt, preferred_element_type=jnp.float32)[0:1]
+            out.append(jnp.where(position[:, block] < live, amounts, 0.0).astype(jnp.bfloat16))
+        return out
+
+    def spread_chunk(i, amounts):
+        cell = cells[i]
+        column = rem_by(cell, nc)
+        tall = div_by(column, WIDE) * nr + div_by(cell, nc)
+        tall = tall.astype(jnp.float32).astype(jnp.bfloat16)
+        short = rem_by(column, WIDE).astype(jnp.float32).astype(jnp.bfloat16)
+        zero, one = jnp.zeros((), jnp.bfloat16), jnp.ones((), jnp.bfloat16)
+        for k in range(PARTS):
+            left, right = [], []
+            for g in range(size // LANES):
+                part = slice(g * LANES, (g + 1) * LANES)
+                spot = slice(k * size + part.start, k * size + part.stop)
+                left.append(
+                    jnp.where(ids[:tall_size] == tall[:, spot], jnp.broadcast_to(amounts[k][:, part], (tall_size, LANES)), zero)
+                )
+                right.append(jnp.where(ids[:WIDE] == short[:, spot], one, zero))
+            product = lax.dot_general(
+                jnp.concatenate(left, axis=1), jnp.concatenate(right, axis=1).astype(jnp.float8_e4m3fn), nt,
+                preferred_element_type=jnp.float32,
+            )
+            totals[k] = product if totals[k] is None else totals[k] + product
+
     for i in range(chunks):
         if i == min(SEND_AT, chunks - 1):
             pack_edges()
@@ -297,30 +330,13 @@
                 op.start()
             spread(ready.at[0], 1, False)
         chunk_loads[i].wait()
-        for op in chunk_loads[i + DEPTH : i + DEPTH + 1] + (edge_loads if i == 0 else []) + (own_loads if i == min(5, chunks - 1) else []):
+        for op in chunk_loads[i + DEPTH : i + DEPTH + 1] + (edge_loads if i == 0 else []) + (own_loads if i == min(8, chunks - 1) else []):
             op.start()
-        position = i * slots + lax.broadcasted_iota(jnp.int32, (1, slots), 1)
-        cell = cells[i]
-        column = rem_by(cell, nc)
-        tall = div_by(column, WIDE) * nr + div_by(cell, nc)
-        tall = tall.astype(jnp.float32).astype(jnp.bfloat16)
-        short = rem_by(column, WIDE).astype(jnp.float32).astype(jnp.bfloat16)
-        zero, one = jnp.zeros((), jnp.bfloat16), jnp.ones((), jnp.bfloat16)
-        for k in range(PARTS):
-            block = slice(k * (slots // PARTS), (k + 1) * (slots // PARTS))
-            amounts = lax.dot_general(wide_weight, pbuf[i, block], nt, preferred_element_type=jnp.float32)[0:1]
-            amounts = jnp.where(position[:, block] < live, amounts, 0.0).astype(jnp.bfloat16)
-            left, right = [], []
-            for g in range(slots // PARTS // LANES):
-                part = slice(g * LANES, (g + 1) * LANES)
-                spot = slice(block.start + part.start, block.start + part.stop)
-                left.append(jnp.where(ids[:tall_size] == tall[:, spot], jnp.broadcast_to(amounts[:, part], (tall_size, LANES)), zero))
-                right.append(jnp.where(ids[:WIDE] == short[:, spot], one, zero))
-            product = lax.dot_general(
-                jnp.concatenate(left, axis=1), jnp.concatenate(right, axis=1).astype(jnp.float8_e4m3fn), nt,
-                preferred_element_type=jnp.float32,
-            )
-            totals[k] = product if totals[k] is None else totals[k] + product
+        ready_amounts = amounts_of(i)
+        if i:
+            spread_chunk(i - 1, waiting_amounts)
+        waiting_amounts = ready_amounts
+    spread_chunk(chunks - 1, waiting_amounts)
     for k in range(PARTS):
         acc_parts[(layer + k) % PARTS] = totals[k].reshape(acc.shape)
     acc[...] = functools.reduce(jnp.add, [acc_parts[k] for k in range(PARTS)])

time: 26.7 us -> 26.3 us (0.985)
  Pallas kernels: 25.2 us -> 24.9 us
    pallas_call x1, Pallas kernels: 23.9 us -> 23.6 us  [per_device(): pl.pallas_call(functools.partial(kernel, sizes, slots), out_shape=(tiled,...]
where the time goes in v5:
time: 26.3 us; the launch traced here: 26.1 us
  Pallas kernels  24.9 us (95%)
  between operations  1.29 us (5%)
    pallas_call x1, Pallas kernels, per_device(): pl.pallas_call(functools.partial(kernel, sizes, slots), out_shape=(tiled,...  23.6 us
    pallas_call x1, Pallas kernels, per_device(): pl.pallas_call(functools.partial(put, half), out_shape=(out, out), in_spe...  1.27 us

profile of v5, /device:TPU:0, one launch (start us, length us, event | category | flops | bytes accessed | tf_op | source)
XLA Modules:
  0.0 26.1 jit_solution(2047368042896359139)
XLA Ops:
  1.3 23.6 %shard_map.95 = (f32[2,3,4,72,128]{4,3,2,1,0:T(8,128)S(1)}, f32[2,3,4,72,128]{4,3,2,1,0:T(8,128)S(1)}) custom-call(bf16[16,1024,256]{2,1,0:T(8,128)(2,1)} %bitcast.3, bf16[2,128]{1,0:T(2,128)(2,1)} %bitcast.5, s32[16,1,1024]{2,1,0:T(1,128)} %bitcast.4, s32[1,1,1]{2,1,0:T(1,128)S(6)} %copy.10.count, f32[3,128,512]{2,1,0:T(8,128)} %metal_in.1, ...), custom_call_target="tpu_custom_call" | custom-call | tf_op jit(solution)/shard_map/pallas_call | solution.py:624
  24.9 1.3 %shard_map.96 = (f32[3,128,512]{2,1,0:T(8,128)}, f32[3,128,512]{2,1,0:T(8,128)}) custom-call(f32[2,3,4,72,128]{4,3,2,1,0:T(8,128)S(1)} %get-tuple-element.4.drop_in, f32[2,3,4,72,128]{4,3,2,1,0:T(8,128)S(1)} %get-tuple-element.5.residual_in), custom_call_target="tpu_custom_call" | custom-call | tf_op jit(solution)/shard_map/pallas_call | solution.py:683
